TPU v7x, 32 devices: a whole 2x2x4 slice. The times are simulated.
32 devices in a mesh: gx: 8 (over z, core), gy: 4 (over y, x).
Axes of the slice: x: 2, y: 2, z: 4, core: 2. Of those that a mesh axis runs over, the one named last changes fastest.
Arguments:
- earlier_heat_field: float32 [6, 1024, 512], P(None, 'gx', 'gy'), may hold values from -6 to 6
- substance_per_voxel: int32 [6, 1024, 512], P(None, 'gx', 'gy'), may hold values from 0 to 7
- patch_wattage_category: int32 [64, 32], P('gx', 'gy'), may hold values from 0 to 63
- planar_coupling: float32 [8], replicated, may hold values from 0.3 to 3
- vertical_coupling_per_substance: float32 [8], replicated, may hold values from 0.05 to 0.5
- heat_mass_ratio: float32 [8], replicated, may hold values from 2e-05 to 0.0002
- wattage_per_category: float32 [64], replicated, may hold values from 2e-06 to 2e-05
Outputs:
- temperature: float32 [6, 1024, 512], P(None, 'gx', 'gy')
All inputs are finite; a program needn't handle non-finite values.
Results may differ from a plain program's by a relative error of at most 0.0003.
Values sent between devices are 32-bit elements; how exact they have to be, the bound alone decides.
A program may use at most 192 MiB of HBM per device.

v0:
```python
import functools

import jax
import jax.numpy as jnp
from jax import lax
from jax.experimental import pallas as pl
from jax.experimental.pallas import tpu as pltpu
from jax.sharding import PartitionSpec as P

TILE = 16
LEVELS = 6
SWEEPS = 2
COARSE_ITERS = 12
LOCAL = 3
FRAME = 64
WIDE = 56
PAD = 8
F32 = jnp.float32
VM = 60 * 1024 * 1024


def up_to(count, step):
    return -(-count // step) * step


def spans(low, high, columns):
    step = max(8, 8 * (4096 // columns // 8) * 2)
    return [(r, min(step, high - r)) for r in range(low, high, step)]


def split_dot(matrix_left, values, matrix_right):
    def parts(x):
        a = x.astype(jnp.bfloat16)
        x = x - a.astype(F32)
        b = x.astype(jnp.bfloat16)
        x = x - b.astype(F32)
        return a, b, x.astype(jnp.bfloat16)

    dot = functools.partial(jnp.dot, preferred_element_type=F32)
    a, b, c = parts(values)
    values = (dot(matrix_left, c) + dot(matrix_left, b)) + dot(matrix_left, a)
    a, b, c = parts(values)
    return (dot(c, matrix_right) + dot(b, matrix_right)) + dot(a, matrix_right)


def pairs(rows, columns, weight, tall):
    r = lax.broadcasted_iota(jnp.int32, (rows, columns), 0)
    c = lax.broadcasted_iota(jnp.int32, (rows, columns), 1)
    hit = (r // 2 == c) if tall else (c // 2 == r)
    return jnp.where(hit, F32(weight), F32(0.0)).astype(jnp.bfloat16)


def restrict(fine, coarse, layers_fine, layers_coarse):
    rf, cf = fine.shape[1] - 2 * PAD, fine.shape[2]
    rc, cc = coarse.shape[1] - 2 * PAD, coarse.shape[2]
    left = pairs(rc, rf, 0.5, False)
    right = pairs(cf, cc, 0.5, True)

    def body(k, carry):
        x = fine[k + layers_fine, PAD : PAD + rf, :]
        coarse[k + layers_coarse, PAD : PAD + rc, :] = split_dot(left, x, right)
        return carry

    lax.fori_loop(0, 6, body, 0)


def prolong_add(coarse, fine):
    rf, cf = fine.shape[1] - 2 * PAD, fine.shape[2]
    rc, cc = coarse.shape[1] - 2 * PAD, coarse.shape[2]
    left = pairs(rf, rc, 1.0, True)
    right = pairs(cc, cf, 1.0, False)

    def body(k, carry):
        x = coarse[k + 1, PAD : PAD + rc, :]
        fine[k + 1, PAD : PAD + rf, :] += split_dot(left, x, right)
        return carry

    lax.fori_loop(0, 6, body, 0)


def build(coef, weights, scale):
    lat, ver, sto = coef
    wr, wc, wv, inv, diag = weights
    rows, columns = lat.shape[1] - 2 * PAD, lat.shape[2]
    half = F32(0.5 * scale)
    wr[...] = jnp.zeros_like(wr)
    wv[0] = jnp.zeros(wv.shape[1:], F32)
    wv[6] = jnp.zeros(wv.shape[1:], F32)

    def faces(k, carry):
        for r, n in spans(PAD, PAD + rows, columns):
            here = lat[k, r : r + n, :]
            wr[k, r : r + n, :] = half * (here + lat[k, r - 1 : r - 1 + n, :])
            wc[k, r : r + n, :] = half * (here + pltpu.roll(here, 1, 1))
        wr[k, PAD + rows : PAD + rows + 8, :] = half * (
            lat[k, PAD + rows : PAD + rows + 8, :]
            + lat[k, PAD + rows - 1 : PAD + rows + 7, :]
        )
        return carry

    lax.fori_loop(0, 6, faces, 0)

    def layer(k, carry):
        for r, n in spans(PAD, PAD + rows, columns):
            wv[k, r : r + n, :] = F32(0.5) * (ver[k, r : r + n, :] + ver[k - 1, r : r + n, :])
        return carry

    lax.fori_loop(1, 6, layer, 0)

    def total(k, carry):
        for r, n in spans(PAD, PAD + rows, columns):
            left = wc[k, r : r + n, :]
            s = sto[k, r : r + n, :]
            d = s + wr[k, r : r + n, :] + wr[k, r + 1 : r + 1 + n, :]
            d = d + left + pltpu.roll(left, columns - 1, 1)
            d = d + wv[k, r : r + n, :] + wv[k + 1, r : r + n, :]
            diag[k, r : r + n, :] = d
            inv[k, r : r + n, :] = jnp.where(s > 0.0, F32(1.0) / jnp.where(s > 0.0, d, 1.0), 0.0)
        return carry

    lax.fori_loop(0, 6, total, 0)


def beside(u, weights, k, r, n, here):
    wr, wc, wv = weights[:3]
    columns = u.shape[2]
    left = wc[k, r : r + n, :]
    summed = wr[k, r : r + n, :] * u[k + 1, r - 1 : r - 1 + n, :]
    summed += wr[k, r + 1 : r + 1 + n, :] * u[k + 1, r + 1 : r + 1 + n, :]
    summed += left * pltpu.roll(here, 1, 1)
    summed += pltpu.roll(left * here, columns - 1, 1)
    summed += wv[k, r : r + n, :] * u[k, r : r + n, :]
    summed += wv[k + 1, r : r + n, :] * u[k + 2, r : r + n, :]
    return summed


def smooth(u, rhs, weights, low, high):
    inv = weights[3]
    columns = u.shape[2]

    def half_sweep(step, carry):
        colour = step % 2

        def layer(k, inner):
            for r, n in spans(PAD + low, PAD + high, columns):
                here = u[k + 1, r : r + n, :]
                new = (rhs[k, r : r + n, :] + beside(u, weights, k, r, n, here)) * inv[
                    k, r : r + n, :
                ]
                odd = lax.broadcasted_iota(jnp.int32, (n, columns), 0)
                odd = (odd + lax.broadcasted_iota(jnp.int32, (n, columns), 1) + k + colour) & 1
                u[k + 1, r : r + n, :] = jnp.where(odd == 0, new, here)
            return inner

        return lax.fori_loop(0, 6, layer, carry)

    lax.fori_loop(0, 2 * SWEEPS, half_sweep, 0)


def residual(u, rhs, weights, out):
    diag = weights[4]
    rows, columns = u.shape[1] - 2 * PAD, u.shape[2]

    def layer(k, carry):
        for r, n in spans(PAD, PAD + rows, columns):
            here = u[k + 1, r : r + n, :]
            out[k, r : r + n, :] = rhs[k, r : r + n, :] - (
                diag[k, r : r + n, :] * here - beside(u, weights, k, r, n, here)
            )
        return carry

    lax.fori_loop(0, 6, layer, 0)


def down_level(index, u, rhs, coef, weights, temp, nxt_rhs, nxt_coef, low, high):
    if index > 0:
        u[...] = jnp.zeros_like(u)
    build(coef, weights, 0.25**index)
    smooth(u, rhs, weights, low, high)
    residual(u, rhs, weights, temp)
    restrict(temp, nxt_rhs, 0, 0)
    for mine, following in zip(coef, nxt_coef):
        following[...] = jnp.zeros_like(following)
        restrict(mine, following, 0, 0)


def down_kernel(x_ref, lat_t, ver_t, sto_t, *refs):
    outs, packed, scratch = refs[: 6 * LOCAL], refs[6 * LOCAL], refs[6 * LOCAL + 1 :]
    level = [outs[6 * i : 6 * i + 6] for i in range(LOCAL)]
    coarse = scratch[5 * LOCAL :]
    own = [scratch[5 * i : 5 * i + 5] for i in range(LOCAL)]
    u, rhs = level[0][:2]
    lat, ver, sto = own[0][:3]
    rows, columns = x_ref.shape[1:]
    for ref in (u, lat):
        ref[...] = jnp.zeros_like(ref)

    def look(k, carry):
        for r, n in spans(0, rows, columns):
            labels = x_ref[k + 6, r : r + n, :]
            a = jnp.zeros((n, columns), F32)
            b, c = a, a
            for m in range(lat_t.shape[0]):
                hit = labels == F32(m + 1)
                a = jnp.where(hit, lat_t[m], a)
                b = jnp.where(hit, ver_t[m], b)
                c = jnp.where(hit, sto_t[m], c)
            t = x_ref[k, r : r + n, :]
            lat[k, r + PAD : r + PAD + n, :] = a
            ver[k, r + PAD : r + PAD + n, :] = b
            sto[k, r + PAD : r + PAD + n, :] = c
            u[k + 1, r + PAD : r + PAD + n, :] = t
            rhs[k, r + PAD : r + PAD + n, :] = c * t
        return carry

    lax.fori_loop(0, 6, look, 0)
    rhs[0, PAD : PAD + rows, :] += x_ref[12]
    for i in range(LOCAL):
        last = i == LOCAL - 1
        size = level[i][0].shape[1] - 2 * PAD
        cut = 8 if i < 2 else 0
        down_level(
            i,
            level[i][0],
            level[i][1],
            own[i][:3],
            level[i][2:6] + own[i][3:4],
            own[i][4],
            coarse[0] if last else level[i + 1][1],
            coarse[1:4] if last else own[i + 1][:3],
            cut,
            size - cut,
        )
    per, h, lanes = packed.shape
    off = FRAME >> LOCAL
    w = lanes * per // 24
    lane = lax.broadcasted_iota(jnp.int32, (h, lanes), 1) // w
    for i in range(per):
        total = jnp.zeros((h, lanes), F32)
        for j in range(24 // per):
            at = j * per + i
            x = coarse[at // 6][at % 6, PAD + off : PAD + off + h, :]
            total = jnp.where(lane == j, pltpu.roll(x, (j * w - off) % lanes, 1), total)
        packed[i] = total


def coarse_kernel(rows_of, g_ref, out_ref, *scratch):
    count = LEVELS - LOCAL
    blocks, per, h, lanes = g_ref.shape
    w = lanes * per // 24
    columns_of = blocks // rows_of
    rows = rows_of * h
    data = [scratch[11 * i : 11 * i + 11] for i in range(count + 1)]
    for j in range(4):
        ref = data[0][(1, 6, 7, 8)[j]]
        ref[...] = jnp.zeros_like(ref)
    lane = lax.broadcasted_iota(jnp.int32, (h, lanes), 1) // w

    def take(gx, carry):
        row = pl.multiple_of(PAD + gx * h, 8)
        for at in range(24):
            j, i = at // per, at % per
            ref = data[0][(1, 6, 7, 8)[at // 6]]
            for start in range(0, columns_of, lanes // w):
                total = jnp.zeros((h, lanes), F32)
                for gy in range(start, min(start + lanes // w, columns_of)):
                    x = g_ref[gx * columns_of + gy, i]
                    x = pltpu.roll(x, ((gy - start - j) * w) % lanes, 1)
                    total = jnp.where(lane == gy - start, x, total)
                ref[at % 6, pl.ds(row, h), start * w : start * w + lanes] = total
        return carry

    lax.fori_loop(0, rows_of, take, 0)
    for i in range(count):
        u, rhs, wr, wc, wv, inv, lat, ver, sto, diag, temp = data[i]
        down_level(
            LOCAL + i, u, rhs, (lat, ver, sto), (wr, wc, wv, inv, diag), temp,
            data[i + 1][1], data[i + 1][6:9], 0, u.shape[1] - 2 * PAD,
        )
    u, rhs, wr, wc, wv, inv, lat, ver, sto, diag, temp = data[count]
    build((lat, ver, sto), (wr, wc, wv, inv, diag), 0.25**LEVELS)
    n, columns = u.shape[1] - 2 * PAD, u.shape[2]
    u[...] = jnp.zeros_like(u)
    mid = slice(PAD, PAD + n)

    def summed(x):
        x = jnp.sum(x, axis=0)
        return jnp.sum(jnp.sum(x, axis=0, keepdims=True), axis=1, keepdims=True)

    r0 = rhs[:, mid, :]
    z0 = r0 * inv[:, mid, :]
    u[1:7, mid, :] = z0
    temp[:, mid, :] = r0
    lat[:, mid, :] = jnp.zeros_like(r0)

    def step(_, rz):
        p = u[1:7, mid, :]
        image = jnp.stack(
            [diag[k, mid, :] * p[k] - beside(u, (wr, wc, wv), k, PAD, n, p[k]) for k in range(6)]
        )
        alpha = rz / summed(p * image)
        lat[:, mid, :] += alpha[None] * p
        r = temp[:, mid, :] - alpha[None] * image
        temp[:, mid, :] = r
        z = r * inv[:, mid, :]
        rz_new = summed(r * z)
        u[1:7, mid, :] = z + (rz_new / rz)[None] * p
        return rz_new

    lax.fori_loop(0, COARSE_ITERS, step, summed(r0 * z0))
    u[1:7, mid, :] = lat[:, mid, :]
    for i in reversed(range(count)):
        u, rhs, wr, wc, wv, inv = data[i][:6]
        prolong_add(data[i + 1][0], u)
        smooth(u, rhs, (wr, wc, wv, inv), 0, u.shape[1] - 2 * PAD)
    u = data[0][0]

    def give(k, carry):
        out_ref[k] = u[k + 1, PAD : PAD + out_ref.shape[1], :]
        return carry

    lax.fori_loop(0, 6, give, 0)


def up_kernel(e_ref, *refs):
    ins = refs[: 6 * LOCAL]
    out_ref = refs[6 * LOCAL]
    us = refs[6 * LOCAL + 1 :]
    correction = e_ref
    for i in reversed(range(LOCAL)):
        u, rhs, wr, wc, wv, inv = ins[6 * i : 6 * i + 6]
        mine = us[i]
        mine[...] = u[...]
        prolong_add(correction, mine)
        size = u.shape[1] - 2 * PAD
        cut = (56, 24, 8)[i]
        smooth(mine, rhs, (wr, wc, wv, inv), cut, size - cut)
        correction = mine
    rows, columns = out_ref.shape[1:]
    wide = correction.shape[2]

    def give(k, carry):
        x = correction[k + 1, PAD + FRAME : PAD + FRAME + rows, :]
        out_ref[k] = pltpu.roll(x, wide - FRAME, 1)[:, :columns]
        return carry

    lax.fori_loop(0, 6, give, 0)


def extended(block, axis, dim):
    count = lax.axis_size(axis)
    forward = [(i, i + 1) for i in range(count - 1)]
    backward = [(target, source) for source, target in forward]
    size = block.shape[dim]
    low = lax.ppermute(lax.slice_in_dim(block, size - WIDE, None, axis=dim), axis, forward)
    high = lax.ppermute(lax.slice_in_dim(block, 0, WIDE, axis=dim), axis, backward)
    shape = list(block.shape)
    shape[dim] = FRAME - WIDE
    edge = jnp.zeros(shape, block.dtype)
    return jnp.concatenate([edge, low, block, high, edge], axis=dim)


def lookup(labels, entries):
    summed = jnp.zeros(labels.shape, entries.dtype)
    for number in range(entries.shape[0]):
        summed = summed + jnp.where(labels == number, entries[number], 0.0)
    return summed


def frame(layers, rows, columns):
    return (layers, rows + 2 * PAD, columns)


def on_device(field, substance, patch, planar, vertical, storage, wattage):
    small = lax.optimization_barrier(lookup(patch, wattage))
    tall = jnp.repeat(jnp.eye(patch.shape[0], dtype=F32), TILE, axis=0)
    flat = jnp.repeat(jnp.eye(patch.shape[1], dtype=F32), TILE, axis=1)
    exact = functools.partial(jnp.dot, precision=lax.Precision.HIGHEST)
    heat = exact(exact(tall, small), flat)
    x = jnp.concatenate([field, substance.astype(F32) + 1.0, heat[None]], 0)
    x = extended(extended(x, "gy", 2), "gx", 1)
    local_rows, local_cols = field.shape[1:]
    vmem = pl.BlockSpec(memory_space=pltpu.VMEM)
    smem = pl.BlockSpec(memory_space=pltpu.SMEM)
    params = pltpu.CompilerParams(vmem_limit_bytes=VM)
    dims = []
    for i in range(LOCAL + 1):
        dims.append(
            (
                up_to((local_rows + 2 * FRAME) >> i, 8),
                up_to((local_cols + 2 * FRAME) >> i, 128),
            )
        )
    shapes, scratch = [], []
    for i in range(LOCAL):
        shapes += [jax.ShapeDtypeStruct(frame(n, *dims[i]), F32) for n in (8, 6, 6, 6, 7, 6)]
        scratch += [pltpu.VMEM(frame(6, *dims[i]), F32) for _ in range(5)]
    scratch += [pltpu.VMEM(frame(6, *dims[LOCAL]), F32) for _ in range(4)]
    h, w = local_rows >> LOCAL, local_cols >> LOCAL
    off = FRAME >> LOCAL
    lanes = dims[LOCAL][1]
    result = pl.pallas_call(
        down_kernel,
        out_shape=shapes + [jax.ShapeDtypeStruct((24 * w // lanes, h, lanes), F32)],
        in_specs=[vmem] + [smem] * 3,
        out_specs=[vmem] * (6 * LOCAL + 1),
        scratch_shapes=scratch,
        compiler_params=params,
    )(x, planar, vertical, storage)
    levels, mine = result[: 6 * LOCAL], result[6 * LOCAL]
    nx, ny = lax.axis_size("gx"), lax.axis_size("gy")
    whole = lax.all_gather(mine, ("gx", "gy"), axis=0, tiled=False)
    sizes = [
        (up_to(((nx * h) >> i) + 1, 8), up_to(((ny * w) >> i) + 1, 128))
        for i in range(LEVELS - LOCAL + 1)
    ]
    scratch = []
    for size in sizes:
        scratch += [
            pltpu.VMEM(frame(n, *size), F32) for n in (8, 6, 6, 6, 7, 6, 6, 6, 6, 6, 6)
        ]
    solved = pl.pallas_call(
        functools.partial(coarse_kernel, nx),
        out_shape=jax.ShapeDtypeStruct((6,) + sizes[0], F32),
        in_specs=[vmem],
        out_specs=vmem,
        scratch_shapes=scratch,
        compiler_params=params,
    )(whole)
    solved = jnp.pad(solved, ((1, 1), (off, off), (off, off)))
    zero = jnp.int32(0)
    window = lax.dynamic_slice(
        solved,
        (zero, lax.axis_index("gx") * h, lax.axis_index("gy") * w),
        (8, h + 2 * off, w + 2 * off),
    )
    r3, c3 = dims[LOCAL]
    window = jnp.pad(window, ((0, 0), (PAD, PAD), (0, c3 - (w + 2 * off))))
    return pl.pallas_call(
        up_kernel,
        out_shape=jax.ShapeDtypeStruct(field.shape, F32),
        in_specs=[vmem] * (1 + 6 * LOCAL),
        out_specs=vmem,
        scratch_shapes=[pltpu.VMEM(frame(8, *dims[i]), F32) for i in range(LOCAL)],
        compiler_params=params,
    )(window, *levels)


def solution(mesh):
    placed = (P(None, "gx", "gy"), P(None, "gx", "gy"), P("gx", "gy"), P(), P(), P(), P())
    return jax.shard_map(
        on_device, mesh=mesh, in_specs=placed, out_specs=P(None, "gx", "gy"), check_vma=False
    )
```

profile of v0, /device:TPU:0, one launch (start us, length us, event | category | flops | bytes accessed | tf_op | source)
XLA Modules:
  0.0 304.3 jit_solution(2554822984635645136)
XLA Ops:
  0.0 2.1 fusion.3
  2.1 2.1 fusion.5
  4.1 2.1 fusion.4
  6.2 1.6 fusion.6
  7.8 40.6 %select_add_fusion = f32[8,8]{1,0:T(8,128)S(1)} fusion(s32[8,8]{1,0:T(8,128)} %param.9, f32[]{:T(128)} %bitcast.64, f32[]{:T(128)} %bitcast.63, f32[]{:T(128)} %bitcast.62, f32[]{:T(128)} %bitcast.61, f32[]{:T(128)} %bitcast.60, f32[]{:T(128)} %bitcast.59, f32[]{:T(128)} %bitcast.58, f32[]{:T(128)} %bitcast.57, f32[]{:T(128)} %bitcast.56, f32[]{:T(128)} %bitcast.55, ...), kind=kLoop, calls=%fused_computation.9 | loop fusion | flops 12224 | bytes 768 | tf_op jit(solution)/shard_map/add | solution.py:366
  48.6 1.0 convert_add_fusion
  49.6 0.2 fusion.7
  50.0 1.1 pad_maximum_fusion
  51.1 0.3 fusion.2
  51.4 0.3 copy.10
  51.7 4.9 %collective-permute-start = (f32[13,128,56]{1,2,0:T(8,128)S(1)}, f32[13,128,56]{1,2,0:T(8,128)S(1)}, u32[]{:S(2)}, u32[]{:S(2)}) collective-permute-start(f32[13,128,56]{1,2,0:T(8,128)S(1)} %copy.10), channel_id=1, source_target_pairs={{0,1},{1,2},{2,3},{4,5},{5,6},{6,7},{8,9},{9,10},{10,11},{12,13},{... | collective-permute-start | bytes 1118216 | tf_op jit(solution)/shard_map/ppermute | solution.py:355
  56.6 0.3 copy.11
  56.9 1.3 collective-permute-start.1
  58.2 6.3 %collective-permute-done = f32[13,128,56]{1,2,0:T(8,128)S(1)} collective-permute-done((f32[13,128,56]{1,2,0:T(8,128)S(1)}, f32[13,128,56]{1,2,0:T(8,128)S(1)}, u32[]{:S(2)}, u32[]{:S(2)}) %collective-permute-start) | collective-permute-done | bytes 372768 | tf_op jit(solution)/shard_map/ppermute | solution.py:355
  64.5 1.2 copy.12
  65.7 8.7 %collective-permute-done.1 = f32[13,128,56]{1,2,0:T(8,128)S(1)} collective-permute-done((f32[13,128,56]{1,2,0:T(8,128)S(1)}, f32[13,128,56]{1,2,0:T(8,128)S(1)}, u32[]{:S(2)}, u32[]{:S(2)}) %collective-permute-start.1) | collective-permute-done | bytes 372768 | tf_op jit(solution)/shard_map/ppermute | solution.py:356
  74.4 1.2 copy.13
  75.7 3.1 %concatenate.10 = f32[13,128,256]{2,1,0:T(8,128)S(1)} concatenate(f32[13,128,8]{2,1,0:T(8,128)S(1)} %broadcast_in_dim.276, f32[13,128,56]{2,1,0:T(8,128)} %copy.12, f32[13,128,128]{2,1,0:T(8,128)S(1)} %pad_maximum_fusion, f32[13,128,56]{2,1,0:T(8,128)} %copy.13, f32[13,128,8]{2,1,0:T(8,128)S(1)} %broadcast_in_dim.276), dimensions={2} | concatenate | bytes 3407872 | tf_op jit(solution)/shard_map/concatenate | solution.py:360
  78.8 1.0 fusion.1
  79.9 2.2 collective-permute-start.2
  82.0 1.3 collective-permute-start.3
  83.3 0.7 broadcast_dynamic-update-slice_fusion
  84.0 2.1 constant_dynamic-update-slice_fusion.2
  86.1 1.4 constant_dynamic-update-slice_fusion.1
  87.5 0.9 constant_dynamic-update-slice_fusion
  88.5 0.7 broadcast_dynamic-update-slice_fusion.1.x_ref
  89.1 53.1 %shard_map.73 = (f32[8,272,256]{2,1,0:T(8,128)}, f32[6,272,256]{2,1,0:T(8,128)}, f32[6,272,256]{2,1,0:T(8,128)}, f32[6,272,256]{2,1,0:T(8,128)}, f32[7,272,256]{...) custom-call(f32[13,256,256]{2,1,0:T(8,128)} %broadcast_dynamic-updat, ...), custom_call_target="tpu_custom_call" | custom-call | tf_op jit(solution)/shard_map/pallas_call | solution.py:402
  142.3 79.0 %all-gather = f32[96,16,128]{2,1,0:T(8,128)} all-gather(f32[3,16,128]{2,1,0:T(8,128)} %get-tuple-element.24), channel_id=2, replica_groups=mesh['gx'=8,'gy'=4] {'gx','gy'}, dimensions={0}, use_global_device_ids=true | all-gather | bytes 811008 | tf_op jit(solution)/shard_map/all_gather | solution.py:412
  221.3 58.9 %shard_map.74 = f32[6,136,128]{2,1,0:T(8,128)} custom-call(f32[32,3,16,128]{3,2,1,0:T(8,128)} %bitcast.72), custom_call_target="tpu_custom_call" | custom-call | tf_op jit(solution)/shard_map/pallas_call | solution.py:422
  280.2 1.0 pad_dynamic-slice_fusion
  281.1 0.7 pad.9.e_ref
  281.8 22.5 %shard_map.75 = f32[6,128,128]{2,1,0:T(8,128)} custom-call(f32[8,48,128]{2,1,0:T(8,128)} %pad.9.e_ref, f32[8,272,256]{2,1,0:T(8,128)} %get-tuple-element.25.refs_0_, f32[6,272,256]{2,1,0:T(8,128)} %get-tuple-element.26.refs_1_, f32[6,272,256]{2,1,0:T(8,128)} %get-tuple-element.27.refs_2_, f32[6,272,256]{2,1,0:T(8,128)} %get-tuple-element.28.refs_3_, ...), custom_call_target="tpu_custom_call" | custom-call | tf_op jit(solution)/shard_map/pallas_call | solution.py:439
  (8 shorter events, 0.4 us)
Async XLA Ops:
  51.7 12.8 %collective-permute-start = (f32[13,128,56]{1,2,0:T(8,128)S(1)}, f32[13,128,56]{1,2,0:T(8,128)S(1)}, u32[]{:S(2)}, u32[]{:S(2)}) collective-permute-start(f32[13,128,56]{1,2,0:T(8,128)S(1)} %copy.10), channel_id=1, source_target_pairs={{0,1},{1,2},{2,3},{4,5},{5,6},{6,7},{8,9},{9,10},{10,11},{12,13},{... | collective-permute-start | bytes 1118216 | tf_op jit(solution)/shard_map/ppermute | solution.py:355
  56.9 17.5 %collective-permute-start.1 = (f32[13,128,56]{1,2,0:T(8,128)S(1)}, f32[13,128,56]{1,2,0:T(8,128)S(1)}, u32[]{:S(2)}, u32[]{:S(2)}) collective-permute-start(f32[13,128,56]{1,2,0:T(8,128)S(1)} %copy.11), channel_id=1, source_target_pairs={{1,0},{2,1},{3,2},{5,4},{6,5},{7,6},{9,8},{10,9},{11,10},{13,12},{... | collective-permute-start | bytes 1118216 | tf_op jit(solution)/shard_map/ppermute | solution.py:356
  79.9 4.1 %collective-permute-start.2 = (f32[13,56,256]{2,1,0:T(8,128)}, f32[13,56,256]{2,1,0:T(8,128)}, u32[]{:S(2)}, u32[]{:S(2)}) collective-permute-start(f32[13,56,256]{2,1,0:T(8,128)} %get-tuple-element.44), channel_id=1, source_target_pairs={{0,4},{4,8},{8,12},{12,16},{16,20},{20,24},{24,28},{1,5},{5,9},{9,... | collective-permute-start | bytes 2236424 | tf_op jit(solution)/shard_map/ppermute | solution.py:355
  82.0 5.5 %collective-permute-start.3 = (f32[13,56,256]{2,1,0:T(8,128)S(1)}, f32[13,56,256]{2,1,0:T(8,128)S(1)}, u32[]{:S(2)}, u32[]{:S(2)}) collective-permute-start(f32[13,56,256]{2,1,0:T(8,128)S(1)} %get-tuple-element.43), channel_id=1, source_target_pairs={{4,0},{8,4},{12,8},{16,12},{20,16},{24,20},{28,24},{5,1},{9,5},{13... | collective-permute-start | bytes 2236424 | tf_op jit(solution)/shard_map/ppermute | solution.py:356
where the time goes:
time: 305 us; the launch traced here: 304 us
  Pallas kernels  135 us (44%)
  blocking collectives  79 us (26%)
  other arithmetic  42.7 us (14%)
  local copies, waits for them, and re-layouts  22.9 us (8%)
  waiting for transfers between devices  15 us (5%)
  starting transfers between devices  9.61 us (3%)
    all_gather x1, blocking collectives, on_device(): whole = lax.all_gather(mine, ('gx', 'gy'), axis=0, tiled=False)  79 us
    pallas_call x1, Pallas kernels, on_device(): pl.pallas_call(functools.partial(coarse_kernel, nx), out_shape=jax.ShapeD...  58.9 us
    pallas_call x1, Pallas kernels, on_device(): pl.pallas_call(down_kernel, out_shape=shapes + [jax.ShapeDtypeStruct((24...  53.1 us
    add x1, other arithmetic, lookup(): summed = summed + jnp.where(labels == number, entries[number], 0.0)  40.6 us
    pallas_call x1, Pallas kernels, on_device(): pl.pallas_call(up_kernel, out_shape=jax.ShapeDtypeStruct(field.shape, F32...  22.5 us
    ppermute x2, waiting for transfers between devices, extended(): lax.ppermute(lax.slice_in_dim(block, 0, WIDE, axis=dim), axis, backward)  8.7 us
    slice x4, local copies, waits for them, and re-layouts, lookup(): summed = summed + jnp.where(labels == number, entries[number], 0.0)  7.78 us
    ppermute x2, starting transfers between devices, extended(): lax.ppermute(lax.slice_in_dim(block, size - WIDE, None, axis=dim), axis,...  7.05 us
  transfers between devices with their start and end apart: 4, of which 2 were waited for; matrix products, arithmetic and copies ran while one was open for 2% of the time, Pallas kernels for 0%

commit v1 on v0

--- a/solution.py
+++ b/solution.py
@@ -372,7 +372,9 @@
 
 
 def on_device(field, substance, patch, planar, vertical, storage, wattage):
-    small = lax.optimization_barrier(lookup(patch, wattage))
+    levels = lax.broadcasted_iota(patch.dtype, patch.shape + wattage.shape, 2)
+    chosen = jnp.where(patch[:, :, None] == levels, wattage[None, None, :], 0.0)
+    small = lax.optimization_barrier(jnp.sum(chosen, axis=2))
     tall = jnp.repeat(jnp.eye(patch.shape[0], dtype=F32), TILE, axis=0)
     flat = jnp.repeat(jnp.eye(patch.shape[1], dtype=F32), TILE, axis=1)
     exact = functools.partial(jnp.dot, precision=lax.Precision.HIGHEST)

time: 305 us -> 257 us (0.84)
  other arithmetic: 42.7 us -> 2.95 us
  local copies, waits for them, and re-layouts: 22.9 us -> 15.1 us
    add x1 -> x0, other arithmetic: 40.6 us -> none  [lookup(): summed = summed + jnp.where(labels == number, entries[number], 0.0)]
    slice x4 -> x0, local copies, waits for them, and re-layouts: 7.78 us -> none  [lookup(): summed = summed + jnp.where(labels == number, entries[number], 0.0)]
where the time goes in v1:
time: 257 us
  Pallas kernels  134 us (52%)
  blocking collectives  79 us (31%)
  local copies, waits for them, and re-layouts  15.1 us (6%)
  waiting for transfers between devices  15 us (6%)
  starting transfers between devices  9.63 us (4%)
  other arithmetic  2.95 us (1%)
    all_gather x1, blocking collectives, on_device(): whole = lax.all_gather(mine, ('gx', 'gy'), axis=0, tiled=False)  79 us
    pallas_call x1, Pallas kernels, on_device(): pl.pallas_call(functools.partial(coarse_kernel, nx), out_shape=jax.ShapeD...  58.9 us
    pallas_call x1, Pallas kernels, on_device(): pl.pallas_call(down_kernel, out_shape=shapes + [jax.ShapeDtypeStruct((24...  53.1 us
    pallas_call x1, Pallas kernels, on_device(): pl.pallas_call(up_kernel, out_shape=jax.ShapeDtypeStruct(field.shape, F32...  22.5 us
    ppermute x2, waiting for transfers between devices, extended(): lax.ppermute(lax.slice_in_dim(block, 0, WIDE, axis=dim), axis, backward)  8.72 us
    ppermute x2, starting transfers between devices, extended(): lax.ppermute(lax.slice_in_dim(block, size - WIDE, None, axis=dim), axis,...  7.06 us
    ppermute x2, waiting for transfers between devices, extended(): lax.ppermute(lax.slice_in_dim(block, size - WIDE, None, axis=dim), axis,...  6.32 us
  transfers between devices with their start and end apart: 4, of which 2 were waited for; matrix products, arithmetic and copies ran while one was open for 2% of the time, Pallas kernels for 0%

profile of v1, /device:TPU:0, one launch (start us, length us, event | category | flops | bytes accessed | tf_op | source)
XLA Modules:
  0.0 256.9 jit_solution(818452349452310082)
XLA Ops:
  0.0 0.9 select_reduce_fusion
  0.9 0.1 broadcast_in_dim.34
  0.9 0.1 reshape.9
  1.0 1.0 convert_add_fusion
  2.1 0.2 fusion.3
  2.3 0.3 convolution_bitcast_fusion
  2.6 1.1 pad_maximum_fusion
  3.7 0.3 fusion.2
  4.0 0.3 copy.15
  4.3 4.9 %collective-permute-start = (f32[13,128,56]{1,2,0:T(8,128)S(1)}, f32[13,128,56]{1,2,0:T(8,128)S(1)}, u32[]{:S(2)}, u32[]{:S(2)}) collective-permute-start(f32[13,128,56]{1,2,0:T(8,128)S(1)} %copy.15), channel_id=1, source_target_pairs={{0,1},{1,2},{2,3},{4,5},{5,6},{6,7},{8,9},{9,10},{10,11},{12,13},{... | collective-permute-start | bytes 1118216 | tf_op jit(solution)/shard_map/ppermute | solution.py:355
  9.2 0.3 copy.16
  9.4 1.3 collective-permute-start.1
  10.7 6.3 %collective-permute-done = f32[13,128,56]{1,2,0:T(8,128)S(1)} collective-permute-done((f32[13,128,56]{1,2,0:T(8,128)S(1)}, f32[13,128,56]{1,2,0:T(8,128)S(1)}, u32[]{:S(2)}, u32[]{:S(2)}) %collective-permute-start) | collective-permute-done | bytes 372768 | tf_op jit(solution)/shard_map/ppermute | solution.py:355
  17.1 1.2 copy.17
  18.3 8.7 %collective-permute-done.1 = f32[13,128,56]{1,2,0:T(8,128)S(1)} collective-permute-done((f32[13,128,56]{1,2,0:T(8,128)S(1)}, f32[13,128,56]{1,2,0:T(8,128)S(1)}, u32[]{:S(2)}, u32[]{:S(2)}) %collective-permute-start.1) | collective-permute-done | bytes 372768 | tf_op jit(solution)/shard_map/ppermute | solution.py:356
  27.0 1.2 copy.18
  28.2 0.1 broadcast_in_dim.30
  28.3 3.1 %concatenate.10 = f32[13,128,256]{2,1,0:T(8,128)S(1)} concatenate(f32[13,128,8]{2,1,0:T(8,128)S(1)} %broadcast_in_dim.30, f32[13,128,56]{2,1,0:T(8,128)} %copy.17, f32[13,128,128]{2,1,0:T(8,128)S(1)} %pad_maximum_fusion, f32[13,128,56]{2,1,0:T(8,128)} %copy.18, f32[13,128,8]{2,1,0:T(8,128)S(1)} %broadcast_in_dim.30), dimensions={2} | concatenate | bytes 3407872 | tf_op jit(solution)/shard_map/concatenate | solution.py:360
  31.4 1.0 fusion.1
  32.4 2.2 collective-permute-start.2
  34.6 1.3 collective-permute-start.3
  35.9 0.6 broadcast_dynamic-update-slice_fusion
  36.5 2.1 constant_dynamic-update-slice_fusion.2
  38.6 1.4 constant_dynamic-update-slice_fusion.1
  40.0 1.0 constant_dynamic-update-slice_fusion
  41.0 0.6 broadcast_dynamic-update-slice_fusion.1.x_ref
  41.6 53.1 %shard_map.73 = (f32[8,272,256]{2,1,0:T(8,128)}, f32[6,272,256]{2,1,0:T(8,128)}, f32[6,272,256]{2,1,0:T(8,128)}, f32[6,272,256]{2,1,0:T(8,128)}, f32[7,272,256]{...) custom-call(f32[13,256,256]{2,1,0:T(8,128)} %broadcast_dynamic-updat, ...), custom_call_target="tpu_custom_call" | custom-call | tf_op jit(solution)/shard_map/pallas_call | solution.py:404
  94.7 79.0 %all-gather = f32[96,16,128]{2,1,0:T(8,128)} all-gather(f32[3,16,128]{2,1,0:T(8,128)} %get-tuple-element.24), channel_id=2, replica_groups=mesh['gx'=8,'gy'=4] {'gx','gy'}, dimensions={0}, use_global_device_ids=true | all-gather | bytes 811008 | tf_op jit(solution)/shard_map/all_gather | solution.py:414
  173.8 58.9 %shard_map.74 = f32[6,136,128]{2,1,0:T(8,128)} custom-call(f32[32,3,16,128]{3,2,1,0:T(8,128)} %bitcast.8), custom_call_target="tpu_custom_call" | custom-call | tf_op jit(solution)/shard_map/pallas_call | solution.py:424
  232.7 1.0 pad_dynamic-slice_fusion
  233.7 0.7 pad.9.e_ref
  234.4 22.5 %shard_map.75 = f32[6,128,128]{2,1,0:T(8,128)} custom-call(f32[8,48,128]{2,1,0:T(8,128)} %pad.9.e_ref, f32[8,272,256]{2,1,0:T(8,128)} %get-tuple-element.25.refs_0_, f32[6,272,256]{2,1,0:T(8,128)} %get-tuple-element.26.refs_1_, f32[6,272,256]{2,1,0:T(8,128)} %get-tuple-element.27.refs_2_, f32[6,272,256]{2,1,0:T(8,128)} %get-tuple-element.28.refs_3_, ...), custom_call_target="tpu_custom_call" | custom-call | tf_op jit(solution)/shard_map/pallas_call | solution.py:441
  (4 shorter events, 0.0 us)
Async XLA Ops:
  4.3 12.8 %collective-permute-start = (f32[13,128,56]{1,2,0:T(8,128)S(1)}, f32[13,128,56]{1,2,0:T(8,128)S(1)}, u32[]{:S(2)}, u32[]{:S(2)}) collective-permute-start(f32[13,128,56]{1,2,0:T(8,128)S(1)} %copy.15), channel_id=1, source_target_pairs={{0,1},{1,2},{2,3},{4,5},{5,6},{6,7},{8,9},{9,10},{10,11},{12,13},{... | collective-permute-start | bytes 1118216 | tf_op jit(solution)/shard_map/ppermute | solution.py:355
  9.4 17.5 %collective-permute-start.1 = (f32[13,128,56]{1,2,0:T(8,128)S(1)}, f32[13,128,56]{1,2,0:T(8,128)S(1)}, u32[]{:S(2)}, u32[]{:S(2)}) collective-permute-start(f32[13,128,56]{1,2,0:T(8,128)S(1)} %copy.16), channel_id=1, source_target_pairs={{1,0},{2,1},{3,2},{5,4},{6,5},{7,6},{9,8},{10,9},{11,10},{13,12},{... | collective-permute-start | bytes 1118216 | tf_op jit(solution)/shard_map/ppermute | solution.py:356
  32.4 4.1 %collective-permute-start.2 = (f32[13,56,256]{2,1,0:T(8,128)}, f32[13,56,256]{2,1,0:T(8,128)}, u32[]{:S(2)}, u32[]{:S(2)}) collective-permute-start(f32[13,56,256]{2,1,0:T(8,128)} %get-tuple-element.44), channel_id=1, source_target_pairs={{0,4},{4,8},{8,12},{12,16},{16,20},{20,24},{24,28},{1,5},{5,9},{9,... | collective-permute-start | bytes 2236424 | tf_op jit(solution)/shard_map/ppermute | solution.py:355
  34.6 5.4 %collective-permute-start.3 = (f32[13,56,256]{2,1,0:T(8,128)S(1)}, f32[13,56,256]{2,1,0:T(8,128)S(1)}, u32[]{:S(2)}, u32[]{:S(2)}) collective-permute-start(f32[13,56,256]{2,1,0:T(8,128)S(1)} %get-tuple-element.43), channel_id=1, source_target_pairs={{4,0},{8,4},{12,8},{16,12},{20,16},{24,20},{28,24},{5,1},{9,5},{13... | collective-permute-start | bytes 2236424 | tf_op jit(solution)/shard_map/ppermute | solution.py:356

commit v2 on v0

v2 whole, which is shorter than its diff:
```python
import functools

import jax
import jax.numpy as jnp
from jax import lax
from jax.experimental import pallas as pl
from jax.experimental.pallas import tpu as pltpu
from jax.sharding import PartitionSpec as P

TILE = 16
LEVELS = 6
COARSE_ITERS = 12
LOCAL = 3
HALO = 8
BASE = 16
LEFT = 16
LANES = 128
F32 = jnp.float32
VM = 63 * 1024 * 1024
MESH = pl.DeviceIdType.MESH
SIDES = ((-1, 0), (1, 0), (0, -1), (0, 1), (-1, -1), (-1, 1), (1, -1), (1, 1))


def up_to(count, step):
    return -(-count // step) * step


def spans(low, high, columns):
    step = max(8, 48 * LANES // columns // 8 * 8)
    return [(r, min(step, high - r)) for r in range(low, high, step)]


def lane_of(shape):
    return lax.broadcasted_iota(jnp.int32, shape, len(shape) - 1)


def row_of(shape):
    return lax.broadcasted_iota(jnp.int32, shape, 0)


def split_dot(values, matrix, terms=3):
    total = None
    pieces = []
    for _ in range(terms):
        piece = values.astype(jnp.bfloat16)
        values = values - piece.astype(F32)
        pieces.append(piece)
    for piece in reversed(pieces):
        part = jnp.dot(piece, matrix, preferred_element_type=F32)
        total = part if total is None else total + part
    return total


def chosen(hit):
    return jnp.where(hit, F32(1.0), F32(0.0)).astype(jnp.bfloat16)


def near(dx, dy):
    ok = None
    for axis, step in (("gx", dx), ("gy", dy)):
        if step == 0:
            continue
        at = lax.axis_index(axis)
        this = (at + step < lax.axis_size(axis)) if step > 0 else (at + step >= 0)
        ok = this if ok is None else jnp.logical_and(ok, this)
    return ok


class Exchange:
    def __init__(self, width, rows, count, row_refs):
        self.width, self.rows, self.count = width, rows, count
        self.per = LANES // width
        self.packs = -(-count // self.per)
        self.row_refs = row_refs

    def scratch(self):
        packed = pltpu.VMEM((2, self.packs, self.rows, LANES), F32)
        landed = pltpu.VMEM((2, self.packs, self.rows + 2 * HALO, LANES), F32)
        tops = [pltpu.VMEM((2, n, HALO, LANES), F32) for n in self.row_refs]
        sems = pltpu.SemaphoreType.DMA((6 + 2 * len(self.row_refs),))
        return [packed, landed, sems, sems] + tops

    def bind(self, refs):
        self.packed, self.landed, self.send, self.recv = refs[:4]
        self.tops = refs[4 : 4 + len(self.row_refs)]
        return refs[4 + len(self.row_refs) :]

    def clear(self):
        self.landed[...] = jnp.zeros_like(self.landed)
        for top in self.tops:
            top[...] = jnp.zeros_like(top)

    def copies(self, sources):
        n = self.rows
        gx, gy = lax.axis_index("gx"), lax.axis_index("gy")
        out = []
        at = 0

        def add(dx, dy, source, target):
            nonlocal at
            out.append((dx, dy, source, target, at))
            at += 1

        for dy, side in ((1, 0), (-1, 1)):
            packed = self.packed.at[side]
            landed = self.landed.at[side]
            add(0, dy, packed, landed.at[:, HALO : HALO + n, :])
            add(1, dy, packed.at[:, n - HALO : n, :], landed.at[:, 0:HALO, :])
            add(-1, dy, packed.at[:, 0:HALO, :], landed.at[:, HALO + n : n + 2 * HALO, :])
        for source, top in zip(sources, self.tops):
            add(1, 0, source.at[:, BASE + n - HALO : BASE + n, :], top.at[0])
            add(-1, 0, source.at[:, BASE : BASE + HALO, :], top.at[1])
        made = []
        for dx, dy, source, target, i in out:
            copy = pltpu.make_async_remote_copy(
                src_ref=source,
                dst_ref=target,
                send_sem=self.send.at[i],
                recv_sem=self.recv.at[i],
                device_id=(gx + dx, gy + dy),
                device_id_type=MESH,
            )
            made.append((dx, dy, copy))
        return made

    def start(self, planes, sources):
        w = self.width
        n = self.rows
        for pack in range(self.packs):
            group = planes[pack * self.per : (pack + 1) * self.per]
            for r, m in spans(0, n, LANES):
                lane = lane_of((m, LANES)) // w
                right = jnp.zeros((m, LANES), F32)
                left = right
                for p, (ref, where) in enumerate(group):
                    x = ref[where + (slice(BASE + r, BASE + r + m),)]
                    hit = lane == p
                    a = pltpu.roll(x, (p * w - (LEFT + 64 - w)) % LANES, 1)
                    b = pltpu.roll(x, (p * w - LEFT) % LANES, 1)
                    right = jnp.where(hit, a, right)
                    left = jnp.where(hit, b, left)
                self.packed[0, pack, r : r + m, :] = right
                self.packed[1, pack, r : r + m, :] = left
        self.sources = sources
        for dx, dy, copy in self.copies(sources):
            pl.when(near(dx, dy))(copy.start)

    def finish(self):
        for dx, dy, copy in self.copies(self.sources):
            pl.when(near(dx, dy))(copy.wait_send)
            pl.when(near(-dx, -dy))(copy.wait_recv)

    def unpack(self, planes, tops, targets):
        w = self.width
        n = self.rows
        for i, (ref, where) in enumerate(planes):
            pack, p = i // self.per, i % self.per
            target, place = targets[i]
            pieces = [(0, HALO, 0)]
            pieces += [(HALO + r, m, None) for r, m in spans(0, n, LANES)]
            pieces += [(HALO + n, HALO, 1)]
            for r, m, side in pieces:
                if side is None:
                    x = ref[where + (slice(BASE - HALO + r, BASE - HALO + r + m),)]
                else:
                    top, plane = tops[i]
                    x = top[side, plane]
                lane = lane_of((m, LANES))
                a = pltpu.roll(self.landed[0, pack, r : r + m, :], (LEFT - w - p * w) % LANES, 1)
                b = pltpu.roll(self.landed[1, pack, r : r + m, :], (LEFT + 64 - p * w) % LANES, 1)
                x = jnp.where((lane >= LEFT - w) & (lane < LEFT), a, x)
                x = jnp.where((lane >= LEFT + 64) & (lane < LEFT + 64 + w), b, x)
                target[place + (slice(BASE - HALO + r, BASE - HALO + r + m),)] = x


def build(coef, wr, wc, wv, scale, gap, low, high):
    columns = coef.shape[2]
    half = F32(0.5 * scale)

    def faces(k, carry):
        for r, n in spans(low, high, columns):
            lane = lane_of((n, columns))
            here = coef[k, r : r + n, :]
            wr[k, r : r + n, :] = half * (here + coef[k, r - 1 : r - 1 + n, :])
            before = jnp.where(lane < gap, 0.0, pltpu.roll(here, gap, 1))
            wc[k, r : r + n, :] = jnp.where(lane < gap, 0.0, half * (here + before))
        here = coef[k, high : high + 8, :]
        wr[k, high : high + 8, :] = half * (here + coef[k, high - 1 : high + 7, :])
        for r, n in spans(low, high, columns):
            inside = F32(0.5) * (coef[6 + k, r : r + n, :] + coef[5 + k, r : r + n, :])
            wv[k, r : r + n, :] = jnp.where(k > 0, inside, 0.0)
        return carry

    lax.fori_loop(0, 6, faces, 0)

    def total(k, carry):
        for r, n in spans(low, high, columns):
            lane = lane_of((n, columns))
            here = coef[k, r : r + n, :]
            before = jnp.where(lane < gap, 0.0, pltpu.roll(here, gap, 1))
            after = jnp.where(lane >= columns - gap, 0.0, pltpu.roll(here, columns - gap, 1))
            s = coef[12 + k, r : r + n, :]
            d = s + wr[k, r : r + n, :] + wr[k, r + 1 : r + 1 + n, :]
            d = d + half * (here + before) + half * (here + after)
            d = d + wv[k, r : r + n, :] + wv[k + 1, r : r + n, :]
            coef[12 + k, r : r + n, :] = d
            coef[6 + k, r : r + n, :] = jnp.where(
                s > 0.0, F32(1.0) / jnp.where(s > 0.0, d, 1.0), 0.0
            )
        return carry

    lax.fori_loop(0, 6, total, 0)


def beside(u, wr, wc, wv, gap, k, r, n, here):
    columns = u.shape[2]
    left = wc[k, r : r + n, :]
    summed = wr[k, r : r + n, :] * u[k + 1, r - 1 : r - 1 + n, :]
    summed += wr[k, r + 1 : r + 1 + n, :] * u[k + 1, r + 1 : r + 1 + n, :]
    summed += left * pltpu.roll(here, gap, 1)
    summed += pltpu.roll(left * here, columns - gap, 1)
    summed += wv[k, r : r + n, :] * u[k, r : r + n, :]
    summed += wv[k + 1, r : r + n, :] * u[k + 2, r : r + n, :]
    return summed


def coloured(n, columns, gap, k, colour):
    shape = (n, columns)
    return ((row_of(shape) + lane_of(shape) // gap + k + colour) & 1) == 0


def smooth(level, low, high, fresh):
    u, rhs, coef, wr, wc, wv, gap = level
    columns = u.shape[2]
    if fresh:

        def begin(k, carry):
            for r, n in spans(low, high, columns):
                new = rhs[k, r : r + n, :] * coef[6 + k, r : r + n, :]
                u[k + 1, r : r + n, :] = jnp.where(coloured(n, columns, gap, k, 0), new, 0.0)
            return carry

        lax.fori_loop(0, 6, begin, 0)

    def half_sweep(step, carry):
        def layer(k, inner):
            for r, n in spans(low, high, columns):
                here = u[k + 1, r : r + n, :]
                new = rhs[k, r : r + n, :] + beside(u, wr, wc, wv, gap, k, r, n, here)
                new = new * coef[6 + k, r : r + n, :]
                u[k + 1, r : r + n, :] = jnp.where(coloured(n, columns, gap, k, step), new, here)
            return inner

        return lax.fori_loop(0, 6, layer, carry)

    lax.fori_loop(1 if fresh else 0, 4, half_sweep, 0)


def residual(level, temp, low, high):
    u, rhs, coef, wr, wc, wv, gap = level
    columns = u.shape[2]

    def layer(k, carry):
        for r, n in spans(low, high, columns):
            here = u[k + 1, r : r + n, :]
            left = rhs[k, r : r + n, :] + beside(u, wr, wc, wv, gap, k, r, n, here)
            left = left - coef[12 + k, r : r + n, :] * here
            temp[k, r : r + n, :] = jnp.where(coloured(n, columns, gap, k, 0), left, 0.0)
        return carry

    lax.fori_loop(0, 6, layer, 0)


def left_dot(matrix, values):
    a = values.astype(jnp.bfloat16)
    values = values - a.astype(F32)
    b = values.astype(jnp.bfloat16)
    c = (values - b.astype(F32)).astype(jnp.bfloat16)
    dot = functools.partial(jnp.dot, preferred_element_type=F32)
    return (dot(matrix, c) + dot(matrix, b)) + dot(matrix, a)


def pair_rows(ref, i, start, count):
    if ref.shape[2] > LANES:
        shape = (count, 2 * count)
        return left_dot(chosen(lane_of(shape) // 2 == row_of(shape)), ref[i, start : start + 2 * count, :])
    return ref[i, pl.ds(start, count, 2), :] + ref[i, pl.ds(start + 1, count, 2), :]


def halve(ref, i, start, count, gap):
    x = pair_rows(ref, i, start, count)
    x = (x + pltpu.roll(x, x.shape[1] - gap, 1)) * F32(0.25)
    return jnp.where(lane_of(x.shape) % (2 * gap) == 0, x, 0.0)


def restrict(fine, coarse, planes, low_fine, low_coarse, count, gap):
    def body(i, carry):
        coarse[i, low_coarse : low_coarse + count, :] = halve(fine, i, low_fine, count, gap)
        return carry

    lax.fori_loop(0, planes, body, 0)


def prolong(coarse, fine, low, count, to, gap):
    def body(k, carry):
        x = coarse[k + 1, low : low + count, :]
        if gap:
            x = x + pltpu.roll(x, gap, 1)
        if x.shape[1] > LANES:
            shape = (2 * count, count)
            twice = left_dot(chosen(row_of(shape) // 2 == lane_of(shape)), x)
            fine[k + 1, to : to + 2 * count, :] += twice
            return carry
        fine[k + 1, pl.ds(to, count, 2), :] += x
        fine[k + 1, pl.ds(to + 1, count, 2), :] += x
        return carry

    lax.fori_loop(0, 6, body, 0)


def turned(x, even):
    return jnp.where(even, pltpu.roll(x, 1, 1), pltpu.roll(x, LANES - 1, 1))


def even_of(n, k, colour):
    return ((row_of((n, LANES)) + k + colour) & 1) == 0


def look(lab, coef, tables, low, high):
    def body(i, carry):
        for r, n in spans(low, high, LANES):
            labels = lab[i, r : r + n, :]
            found = [jnp.zeros((n, LANES), F32)] * 3
            for m in range(tables[0].shape[0]):
                hit = labels == F32(m + 1)
                found = [jnp.where(hit, t[m], x) for t, x in zip(tables, found)]
            for t in range(3):
                coef[12 * t + i, r : r + n, :] = found[t]
        return carry

    lax.fori_loop(0, 12, body, 0)


def build_pair(coef, lab, u, rhs, face, side, low, high):
    half = F32(0.5)

    def faces(k, carry):
        for r, n in spans(low, high, LANES):
            here = coef[k, r : r + n, :]
            other = coef[6 + k, r : r + n, :]
            face[k, r : r + n, :] = half * (here + coef[6 + k, r - 1 : r - 1 + n, :])
            face[6 + k, r : r + n, :] = half * (here + coef[6 + k, r + 1 : r + 1 + n, :])
            face[12 + k, r : r + n, :] = half * (here + other)
            face[18 + k, r : r + n, :] = half * (here + turned(other, even_of(n, k, 0)))
            v = coef[12 + k, r : r + n, :]
            below = half * (v + coef[17 + k, r : r + n, :])
            above = half * (v + coef[19 + k, r : r + n, :])
            side[k + 1, r : r + n, :] = jnp.where(k > 0, below, 0.0)
            side[9 + k, r : r + n, :] = jnp.where(k < 5, above, 0.0)
        return carry

    lax.fori_loop(0, 6, faces, 0)

    def totals(k, carry):
        for r, n in spans(low, high, LANES):
            for colour in (0, 1):
                s = coef[24 + 6 * colour + k, r : r + n, :]
                if colour == 0:
                    d = s + face[k, r : r + n, :] + face[6 + k, r : r + n, :]
                    d = d + face[12 + k, r : r + n, :] + face[18 + k, r : r + n, :]
                    d = d + side[k + 1, r : r + n, :] + side[9 + k, r : r + n, :]
                else:
                    d = s + face[6 + k, r - 1 : r - 1 + n, :] + face[k, r + 1 : r + 1 + n, :]
                    d = d + face[12 + k, r : r + n, :]
                    d = d + turned(face[18 + k, r : r + n, :], even_of(n, k, 1))
                    d = d + side[8 + k, r : r + n, :] + side[k + 2, r : r + n, :]
                heat = jnp.where(k == 0, lab[12, r : r + n, :], 0.0)
                rhs[6 * colour + k, r : r + n, :] = s * u[8 * colour + k + 1, r : r + n, :] + heat
                coef[24 + 6 * colour + k, r : r + n, :] = d
                coef[12 + 6 * colour + k, r : r + n, :] = jnp.where(
                    s > 0.0, F32(1.0) / jnp.where(s > 0.0, d, 1.0), 0.0
                )
        return carry

    lax.fori_loop(0, 6, totals, 0)


def beside_pair(u, face, side, colour, k, r, n):
    o = 8 * (1 - colour)
    same = u[o + k + 1, r : r + n, :]
    before = u[o + k + 1, r - 1 : r - 1 + n, :]
    after = u[o + k + 1, r + 1 : r + 1 + n, :]
    even = even_of(n, k, colour)
    summed = face[12 + k, r : r + n, :] * same
    if colour == 0:
        summed += face[k, r : r + n, :] * before + face[6 + k, r : r + n, :] * after
        summed += face[18 + k, r : r + n, :] * turned(same, even)
        summed += side[k + 1, r : r + n, :] * u[o + k, r : r + n, :]
        summed += side[9 + k, r : r + n, :] * u[o + k + 2, r : r + n, :]
    else:
        summed += face[6 + k, r - 1 : r - 1 + n, :] * before
        summed += face[k, r + 1 : r + 1 + n, :] * after
        summed += turned(face[18 + k, r : r + n, :] * same, even)
        summed += side[8 + k, r : r + n, :] * u[o + k, r : r + n, :]
        summed += side[k + 2, r : r + n, :] * u[o + k + 2, r : r + n, :]
    return summed


def smooth_pair(u, rhs, coef, face, side, low, high):
    def sweep(_, carry):
        for colour in (0, 1):

            def layer(k, inner):
                for r, n in spans(low, high, LANES):
                    new = rhs[6 * colour + k, r : r + n, :]
                    new = new + beside_pair(u, face, side, colour, k, r, n)
                    new = new * coef[12 + 6 * colour + k, r : r + n, :]
                    u[8 * colour + k + 1, r : r + n, :] = new
                return inner

            carry = lax.fori_loop(0, 6, layer, carry)
        return carry

    lax.fori_loop(0, 2, sweep, 0)


def residual_pair(u, rhs, coef, face, side, temp, low, high):
    def layer(k, carry):
        for r, n in spans(low, high, LANES):
            left = rhs[k, r : r + n, :] + beside_pair(u, face, side, 0, k, r, n)
            temp[k, r : r + n, :] = left - coef[24 + k, r : r + n, :] * u[k + 1, r : r + n, :]
        return carry

    lax.fori_loop(0, 6, layer, 0)


def greet(waiting):
    barrier = pltpu.get_barrier_semaphore()
    gx, gy = lax.axis_index("gx"), lax.axis_index("gy")
    nx, ny = lax.axis_size("gx"), lax.axis_size("gy")
    if waiting:
        across = jnp.where(gx > 0, 1, 0) + jnp.where(gx < nx - 1, 1, 0)
        along = jnp.where(gy > 0, 1, 0) + jnp.where(gy < ny - 1, 1, 0)
        pl.semaphore_wait(barrier, nx + ny - 2 + across * along)
        return
    for step in range(1, nx):
        other = (lax.rem(gx + step, nx), gy)
        pl.semaphore_signal(barrier, inc=1, device_id=other, device_id_type=MESH)
    for step in range(1, ny):
        other = (gx, lax.rem(gy + step, ny))
        pl.semaphore_signal(barrier, inc=1, device_id=other, device_id_type=MESH)
    for dx, dy in SIDES[4:]:

        @pl.when(near(dx, dy))
        def _(dx=dx, dy=dy):
            other = (gx + dx, gy + dy)
            pl.semaphore_signal(barrier, inc=1, device_id=other, device_id_type=MESH)


def gather_copies(whole, sems, axis):
    size = lax.axis_size(axis)
    gx, gy = lax.axis_index("gx"), lax.axis_index("gy")
    made = []
    for step in range(1, size):
        if axis == "gx":
            target = (lax.rem(gx + step, size), gy)
            source = whole.at[gy, gx]
            origin = whole.at[gy, lax.rem(gx + size - step, size)]
        else:
            target = (gx, lax.rem(gy + step, size))
            source = whole.at[gy]
            origin = whole.at[lax.rem(gy + size - step, size)]
        out = pltpu.make_async_remote_copy(
            src_ref=source, dst_ref=source, send_sem=sems[0].at[step],
            recv_sem=sems[1].at[step], device_id=target, device_id_type=MESH,
        )
        into = pltpu.make_async_remote_copy(
            src_ref=origin, dst_ref=origin, send_sem=sems[0].at[step],
            recv_sem=sems[1].at[step], device_id=target, device_id_type=MESH,
        )
        made.append((out, into))
    return made


def begin(made):
    for out, _ in made:
        out.start()


def end(made):
    for out, into in made:
        out.wait_send()
        into.wait_recv()


def squeeze(planes):
    rows = 6 * LANES
    r = lax.broadcasted_iota(jnp.int32, (rows, LANES), 0)
    c = lax.broadcasted_iota(jnp.int32, (rows, LANES), 1)
    at = (c // 16) * LANES + LEFT + 4 * (c % 16)
    return split_dot(jnp.concatenate(planes, axis=1), chosen(r == at))


def place(whole, targets, h):
    ny, nx = whole.shape[:2]
    wide = min(ny, LANES // 16)

    def body(gx, carry):
        row = pl.multiple_of(8 + gx * h, 8)
        for t, (ref, first) in enumerate(targets):
            for k in range(6):
                for start in range(0, ny, wide):
                    total = jnp.zeros((h, LANES), F32)
                    lane = lane_of((h, LANES)) // 16
                    for gy in range(start, min(start + wide, ny)):
                        x = whole[gy, gx, t * h : (t + 1) * h, :]
                        x = pltpu.roll(x, (16 * (gy - start - k)) % LANES, 1)
                        total = jnp.where(lane == gy - start, x, total)
                    ref[first + k, pl.ds(row, h), start * 16 : start * 16 + LANES] = total
        return carry

    lax.fori_loop(0, nx, body, 0)


def conjugate(level, temp, out):
    u, rhs, coef, wr, wc, wv, gap = level
    n, columns = u.shape[1] - 16, u.shape[2]
    mid = slice(8, 8 + n)

    def summed(x):
        x = jnp.sum(x, axis=0)
        return jnp.sum(jnp.sum(x, axis=0, keepdims=True), axis=1, keepdims=True)

    inv = slice(6, 12)
    r0 = rhs[:, mid, :]
    z0 = r0 * coef[inv, mid, :]
    u[1:7, mid, :] = z0
    temp[:, mid, :] = r0
    out[:, mid, :] = jnp.zeros_like(r0)

    def step(_, rz):
        p = u[1:7, mid, :]
        image = jnp.stack(
            [
                coef[12 + k, mid, :] * p[k] - beside(u, wr, wc, wv, gap, k, 8, n, p[k])
                for k in range(6)
            ]
        )
        alpha = rz / summed(p * image)
        out[:, mid, :] += alpha[None] * p
        r = temp[:, mid, :] - alpha[None] * image
        temp[:, mid, :] = r
        z = r * coef[inv, mid, :]
        rz_new = summed(r * z)
        u[1:7, mid, :] = z + (rz_new / rz)[None] * p
        return rz_new

    lax.fori_loop(0, COARSE_ITERS, step, summed(r0 * z0))
    u[1:7, mid, :] = out[:, mid, :]


def exchanges(n0):
    n1, n2 = n0 // 2, n0 // 4
    return {
        "near": Exchange(4, n0, 25, (12, 13)),
        "coef1": Exchange(8, n1, 18, (18,)),
        "coef2": Exchange(16, n2, 18, (18,)),
        "u0": Exchange(4, n0, 12, (12,)),
        "rhs1": Exchange(8, n1, 6, (6,)),
        "u1": Exchange(8, n1, 6, (6,)),
        "rhs2": Exchange(16, n2, 6, (6,)),
        "u2": Exchange(16, n2, 6, (6,)),
    }


def scratches(n0, nx, ny):
    def planes(n, rows, columns=LANES):
        return pltpu.VMEM((n, rows, columns), F32)

    rows = n0 + 2 * BASE
    shapes = [planes(n, rows) for n in (16, 13, 36, 12, 24, 16, 12)]
    for i in (1, 2):
        r = (n0 >> i) + 2 * BASE
        shapes += [planes(n, r) for n in (8, 6, 18, 6, 6, 7)]
    h = n0 >> LOCAL
    shapes += [pltpu.VMEM((ny, nx, 3 * h, LANES), F32), pltpu.VMEM((ny, nx, h, LANES), F32)]
    shapes += [pltpu.SemaphoreType.DMA((nx,)), pltpu.SemaphoreType.DMA((nx,))] * 2
    shapes += [pltpu.SemaphoreType.DMA((ny,)), pltpu.SemaphoreType.DMA((ny,))] * 2
    columns = up_to(ny * h, LANES)
    for i in range(LEVELS - LOCAL + 1):
        r = ((nx * h) >> i) + 16
        shapes += [planes(n, r, columns) for n in (8, 6, 18, 6, 6, 7)]
    shapes += [planes(6, (nx * h) + 16, columns)]
    return shapes


def whole_kernel(field, labels, patch, lat_t, ver_t, sto_t, wattage, out, *refs):
    n0 = field.shape[1]
    n1, n2, h = n0 // 2, n0 // 4, n0 // 8
    nx, ny = lax.axis_size("gx"), lax.axis_size("gy")
    u0, lab, coef0, rhs0, face, side, lab_own = refs[:7]
    levels = {}
    at = 7
    for i in (1, 2):
        u, rhs, coef, wr, wc, wv = refs[at : at + 6]
        levels[i] = (u, rhs, coef, wr, wc, wv, i)
        at += 6
    gathered_coef, gathered_rhs = refs[at : at + 2]
    sems = refs[at + 2 : at + 10]
    at += 10
    for i in range(LOCAL, LEVELS + 1):
        u, rhs, coef, wr, wc, wv = refs[at : at + 6]
        levels[i] = (u, rhs, coef, wr, wc, wv, 1 << (i - LOCAL))
        at += 6
    temp3 = refs[at]
    rest = refs[at + 1 :]
    ex = exchanges(n0)
    for e in ex.values():
        rest = e.bind(rest)
        e.clear()
    greet(False)
    for ref in (u0, lab, coef0, rhs0, face, side):
        ref[...] = jnp.zeros_like(ref)
    for level in levels.values():
        for ref in level[:6]:
            ref[...] = jnp.zeros_like(ref)

    r = lax.broadcasted_iota(jnp.int32, (n0, 2 * LANES), 0)
    c = lax.broadcasted_iota(jnp.int32, (n0, 2 * LANES), 1)
    spread = chosen(r == 2 * (c % LANES - LEFT) + c // LANES)
    own = slice(BASE, BASE + n0)

    def part(k, carry):
        even = even_of(n0, k, 0)
        both = split_dot(field[k], spread)
        a, b = both[:, :LANES], both[:, LANES:]
        u0[k + 1, own, :] = jnp.where(even, a, b)
        u0[k + 9, own, :] = jnp.where(even, b, a)
        both = split_dot(labels[k].astype(F32) + F32(1.0), spread, 1)
        inside = (lane_of((n0, LANES)) >= LEFT) & (lane_of((n0, LANES)) < LEFT + 64)
        a, b = both[:, :LANES], both[:, LANES:]
        lab[k, own, :] = jnp.where(inside, jnp.where(even, a, b), 0.0)
        lab[k + 6, own, :] = jnp.where(inside, jnp.where(even, b, a), 0.0)
        return carry

    lax.fori_loop(0, 6, part, 0)
    tiles = patch[...]
    small = jnp.zeros(tiles.shape, F32)
    for m in range(wattage.shape[0]):
        small = jnp.where(tiles == m, wattage[m], small)
    th, tw = tiles.shape
    r = lax.broadcasted_iota(jnp.int32, (tw, LANES), 0)
    c = lax.broadcasted_iota(jnp.int32, (tw, LANES), 1)
    flat = chosen((c >= LEFT) & ((c - LEFT) // (TILE // 2) == r))
    heat = split_dot(small, flat)
    for i in range(th):
        lab[12, BASE + i * TILE : BASE + (i + 1) * TILE, :] = jnp.broadcast_to(
            heat[i : i + 1, :], (TILE, LANES)
        )

    fields = [(u0, (1 + k + 8 * c,)) for c in (0, 1) for k in range(6)]
    labs = [(lab, (i,)) for i in range(13)]
    edge = ex["near"]
    stage = lab_own
    for c in (0, 1):
        stage[6 * c : 6 * c + 6, own, :] = u0[1 + 8 * c : 7 + 8 * c, own, :]
    greet(True)
    edge.start(fields + labs, (stage, lab))

    tables = (lat_t, ver_t, sto_t)
    look(lab, coef0, tables, BASE, BASE + n0)
    coef1, coef2 = levels[1][2], levels[2][2]

    def first(i, carry):
        t, k = i // 6, i % 6
        x = pair_rows(coef0, 12 * t + k, BASE, n1) + pair_rows(coef0, 12 * t + 6 + k, BASE, n1)
        coef1[i, BASE : BASE + n1, :] = x * F32(0.25)
        return carry

    lax.fori_loop(0, 18, first, 0)
    restrict(coef1, coef2, 18, BASE, BASE, n2, 1)
    ex["coef1"].start([(coef1, (i,)) for i in range(18)], (coef1,))
    ex["coef2"].start([(coef2, (i,)) for i in range(18)], (coef2,))
    gx, gy = lax.axis_index("gx"), lax.axis_index("gy")
    for t in range(3):
        planes = [halve(coef2, 6 * t + k, BASE, h, 2) for k in range(6)]
        gathered_coef[gy, gx, t * h : (t + 1) * h, :] = squeeze(planes)
    coef_x = gather_copies(gathered_coef, sems[0:2], "gx")
    begin(coef_x)

    edge.finish()
    tops = [(edge.tops[0], i) for i in range(12)] + [(edge.tops[1], i) for i in range(13)]
    edge.unpack(fields + labs, tops, fields + labs)
    lo, hi0, hi1, hi2 = BASE - HALO, BASE + n0 + HALO, BASE + n1 + HALO, BASE + n2 + HALO
    look(lab, coef0, tables, lo, hi0)
    build_pair(coef0, lab, u0, rhs0, face, side, lo, hi0)
    smooth_pair(u0, rhs0, coef0, face, side, lo, hi0)
    temp = coef0
    residual_pair(u0, rhs0, coef0, face, side, temp, BASE, BASE + n0)
    rhs1, rhs2 = levels[1][1], levels[2][1]

    def down(k, carry):
        rhs1[k, BASE : BASE + n1, :] = pair_rows(temp, k, BASE, n1) * F32(0.25)
        return carry

    lax.fori_loop(0, 6, down, 0)
    ex["rhs1"].start([(rhs1, (k,)) for k in range(6)], (rhs1,))
    for c in (0, 1):
        stage[6 * c : 6 * c + 6, own, :] = u0[1 + 8 * c : 7 + 8 * c, own, :]
    ex["u0"].start(fields, (stage,))

    def fill(name, ref, count, first=0):
        e = ex[name]
        e.finish()
        planes = [(ref, (first + i,)) for i in range(count)]
        e.unpack(planes, [(e.tops[0], i) for i in range(count)], planes)

    def weigh(i, low, high):
        u, rhs, coef, wr, wc, wv, gap = levels[i]
        build(coef, wr, wc, wv, 0.25**i, gap, low, high)

    fill("coef1", coef1, 18)
    weigh(1, lo, hi1)
    fill("coef2", coef2, 18)
    weigh(2, lo, hi2)
    end(coef_x)
    coef_y = gather_copies(gathered_coef, sems[4:6], "gy")
    begin(coef_y)

    fill("rhs1", rhs1, 6)
    smooth(levels[1], lo, hi1, True)
    u1 = levels[1][0]
    residual(levels[1], temp, BASE, BASE + n1)
    restrict(temp, rhs2, 6, BASE, BASE, n2, 1)
    ex["rhs2"].start([(rhs2, (k,)) for k in range(6)], (rhs2,))
    ex["u1"].start([(u1, (k + 1,)) for k in range(6)], (u1.at[1:7],))
    end(coef_y)
    coef3 = levels[3][2]
    place(gathered_coef, [(coef3, 0), (coef3, 6), (coef3, 12)], h)

    fill("rhs2", rhs2, 6)
    smooth(levels[2], lo, hi2, True)
    u2 = levels[2][0]
    residual(levels[2], temp, BASE, BASE + n2)
    gathered_rhs[gy, gx] = squeeze([halve(temp, k, BASE, h, 2) for k in range(6)])
    rhs_x = gather_copies(gathered_rhs, sems[2:4], "gx")
    begin(rhs_x)
    ex["u2"].start([(u2, (k + 1,)) for k in range(6)], (u2.at[1:7],))

    sizes = {i: (nx * h) >> (i - LOCAL) for i in range(LOCAL, LEVELS + 1)}
    for i in range(LOCAL, LEVELS):
        restrict(levels[i][2], levels[i + 1][2], 18, 8, 8, sizes[i + 1], levels[i][6])
    end(rhs_x)
    rhs_y = gather_copies(gathered_rhs, sems[6:8], "gy")
    begin(rhs_y)
    for i in range(LOCAL, LEVELS + 1):
        weigh(i, 8, 8 + sizes[i])
    end(rhs_y)
    place(gathered_rhs, [(levels[3][1], 0)], h)

    for i in range(LOCAL, LEVELS):
        smooth(levels[i], 8, 8 + sizes[i], True)
        residual(levels[i], temp3, 8, 8 + sizes[i])
        restrict(temp3, levels[i + 1][1], 6, 8, 8, sizes[i + 1], levels[i][6])
    conjugate(levels[LEVELS], temp3, levels[LEVELS][1])
    for i in reversed(range(LOCAL, LEVELS)):
        prolong(levels[i + 1][0], levels[i][0], 8, sizes[i + 1], 8, levels[i][6])
        smooth(levels[i], 8, 8 + sizes[i], False)

    u3 = levels[3][0]
    columns = u3.shape[2]
    r = lax.broadcasted_iota(jnp.int32, (columns, LANES), 0)
    c = lax.broadcasted_iota(jnp.int32, (columns, LANES), 1)
    hit = ((c & 1) == 0) & (c // 4 - LEFT // 4 + gy * 16 == r)
    widen = chosen(hit)
    fill("u2", u2, 6, 1)

    def window(k, carry):
        x = u3[k + 1, pl.ds(pl.multiple_of(gx * h, 8), h + 16), :]
        x = split_dot(x, widen)
        u2[k + 1, pl.ds(0, h + 16, 2), :] += x
        u2[k + 1, pl.ds(1, h + 16, 2), :] += x
        return carry

    lax.fori_loop(0, 6, window, 0)
    smooth(levels[2], lo, hi2, False)
    fill("u1", u1, 6, 1)
    prolong(u2, u1, lo, n2 + 16, 0, 1)
    smooth(levels[1], lo, hi1, False)
    e = ex["u0"]
    e.finish()
    e.unpack(fields, [(e.tops[0], i) for i in range(12)], fields)

    def up(k, carry):
        x = u1[k + 1, lo : lo + n1 + 16, :]
        for c in (0, 8):
            u0[c + k + 1, pl.ds(0, n1 + 16, 2), :] += x
            u0[c + k + 1, pl.ds(1, n1 + 16, 2), :] += x
        return carry

    lax.fori_loop(0, 6, up, 0)
    smooth_pair(u0, rhs0, coef0, face, side, lo, hi0)

    r = lax.broadcasted_iota(jnp.int32, (2 * LANES, n0), 0)
    c = lax.broadcasted_iota(jnp.int32, (2 * LANES, n0), 1)
    join = chosen(c == 2 * (r % LANES - LEFT) + r // LANES)

    def give(k, carry):
        even = even_of(n0, k, 0)
        red, black = u0[k + 1, own, :], u0[k + 9, own, :]
        both = jnp.concatenate(
            [jnp.where(even, red, black), jnp.where(even, black, red)], axis=1
        )
        out[k] = split_dot(both, join)
        return carry

    lax.fori_loop(0, 6, give, 0)


def on_device(field, substance, patch, planar, vertical, storage, wattage):
    n0 = field.shape[1]
    nx, ny = lax.axis_size("gx"), lax.axis_size("gy")
    vmem = pl.BlockSpec(memory_space=pltpu.VMEM)
    smem = pl.BlockSpec(memory_space=pltpu.SMEM)
    scratch = scratches(n0, nx, ny)
    for e in exchanges(n0).values():
        scratch += e.scratch()
    return pl.pallas_call(
        whole_kernel,
        out_shape=jax.ShapeDtypeStruct(field.shape, F32),
        in_specs=[vmem] * 3 + [smem] * 4,
        out_specs=vmem,
        scratch_shapes=scratch,
        compiler_params=pltpu.CompilerParams(vmem_limit_bytes=VM, has_side_effects=True, collective_id=0),
    )(field, substance, patch, planar, vertical, storage, wattage)


def solution(mesh):
    placed = (P(None, "gx", "gy"), P(None, "gx", "gy"), P("gx", "gy"), P(), P(), P(), P())
    return jax.shard_map(
        on_device, mesh=mesh, in_specs=placed, out_specs=P(None, "gx", "gy"), check_vma=False
    )
```

time: 305 us -> 85.7 us (0.28)
  blocking collectives: 79 us -> 0 us
  Pallas kernels: 135 us -> 83.7 us
  other arithmetic: 42.7 us -> 0 us
  local copies, waits for them, and re-layouts: 22.9 us -> 1.77 us
  waiting for transfers between devices: 15 us -> 0 us
  starting transfers between devices: 9.61 us -> 0 us
    all_gather x1 -> x0, blocking collectives: 79 us -> none  [on_device(): whole = lax.all_gather(mine, ('gx', 'gy'), axis=0, tiled=False)]
    pallas_call x3 -> x1, Pallas kernels: 135 us -> 83.7 us  [on_device(): pl.pallas_call(whole_kernel, out_shape=jax.ShapeDtypeStruct(field.shape,...]
    add x2 -> x0, other arithmetic: 41.7 us -> none  [the longest x1 40.6 us: lookup(): summed = summed + jnp.where(labels == number, entries[number], 0.0)]
    ppermute x4 -> x0, waiting for transfers between devices: 15 us -> none  [the longest x2 8.7 us: extended(): lax.ppermute(lax.slice_in_dim(block, 0, WIDE, axis=dim), axis, backward)]
    slice x8 -> x0, local copies, waits for them, and re-layouts: 9.66 us -> none  [the longest x4 7.78 us: lookup(): summed = summed + jnp.where(labels == number, entries[number], 0.0)]
    ppermute x4 -> x0, starting transfers between devices: 9.61 us -> none  [the longest x2 7.05 us: extended(): lax.ppermute(lax.slice_in_dim(block, size - WIDE, None, axis=dim), axis,...]
    concatenate x2 -> x0, local copies, waits for them, and re-layouts: 3.77 us -> none  [extended(): return jnp.concatenate([edge, low, block, high, edge], axis=dim)]
    unnamed x4 -> x1, local copies, waits for them, and re-layouts: 5.14 us -> 1.77 us
  transfers between devices with their start and end apart: 4 -> 0, of which waited for: 2 -> 0; matrix products, arithmetic and copies ran while one was open for 2% -> 0% of each run, Pallas kernels for 0% -> 0%
where the time goes in v2:
time: 85.7 us; the launch traced here: 85.5 us
  Pallas kernels  83.7 us (98%)
  local copies, waits for them, and re-layouts  1.77 us (2%)
    pallas_call x1, Pallas kernels, on_device(): pl.pallas_call(whole_kernel, out_shape=jax.ShapeDtypeStruct(field.shape,...  83.7 us
    unnamed x1, local copies, waits for them, and re-layouts  1.77 us

profile of v2, /device:TPU:0, one launch (start us, length us, event | category | flops | bytes accessed | tf_op | source)
XLA Modules:
  0.0 85.5 jit_solution(18075749320929007607)
XLA Ops:
  0.0 83.7 %shard_map.73 = f32[6,128,128]{2,1,0:T(8,128)} custom-call(f32[6,128,128]{2,1,0:T(8,128)} %field.1, s32[6,128,128]{2,1,0:T(8,128)} %labels.1, s32[8,8]{1,0:T(8,128)} %patch.1, f32[8]{0:T(128)} %lat_t.1, f32[8]{0:T(128)} %ver_t.1, f32[8]{0:T(128)} %sto_t.1, f32[64]{0:T(128)} %wattage.1), custom_call_target="tpu_custom_call" | custom-call | tf_op jit(solution)/shard_map/pallas_call | solution.py:828
  83.7 1.8 %copy.9 = f32[6,128,128]{2,1,0:T(8,128)} copy(f32[6,128,128]{2,1,0:T(8,128)} %shard_map.73) | data formatting | bytes 786432

commit v3 on v2

--- a/solution.py
+++ b/solution.py
@@ -176,8 +176,8 @@
 def build(coef, wr, wc, wv, scale, gap, low, high):
     columns = coef.shape[2]
     half = F32(0.5 * scale)
-
-    def faces(k, carry):
+    wv[6] = jnp.zeros(wv.shape[1:], F32)
+    for k in range(6):
         for r, n in spans(low, high, columns):
             lane = lane_of((n, columns))
             here = coef[k, r : r + n, :]
@@ -187,13 +187,12 @@
         here = coef[k, high : high + 8, :]
         wr[k, high : high + 8, :] = half * (here + coef[k, high - 1 : high + 7, :])
         for r, n in spans(low, high, columns):
-            inside = F32(0.5) * (coef[6 + k, r : r + n, :] + coef[5 + k, r : r + n, :])
-            wv[k, r : r + n, :] = jnp.where(k > 0, inside, 0.0)
-        return carry
-
-    lax.fori_loop(0, 6, faces, 0)
-
-    def total(k, carry):
+            if k:
+                inside = coef[6 + k, r : r + n, :] + coef[5 + k, r : r + n, :]
+                wv[k, r : r + n, :] = F32(0.5) * inside
+            else:
+                wv[k, r : r + n, :] = jnp.zeros((n, columns), F32)
+    for k in range(6):
         for r, n in spans(low, high, columns):
             lane = lane_of((n, columns))
             here = coef[k, r : r + n, :]
@@ -207,20 +206,19 @@
             coef[6 + k, r : r + n, :] = jnp.where(
                 s > 0.0, F32(1.0) / jnp.where(s > 0.0, d, 1.0), 0.0
             )
-        return carry
-
-    lax.fori_loop(0, 6, total, 0)
 
 
 def beside(u, wr, wc, wv, gap, k, r, n, here):
     columns = u.shape[2]
     left = wc[k, r : r + n, :]
-    summed = wr[k, r : r + n, :] * u[k + 1, r - 1 : r - 1 + n, :]
+    summed = left * pltpu.roll(here, gap, 1)
+    summed += pltpu.roll(left * here, columns - gap, 1)
+    summed += wr[k, r : r + n, :] * u[k + 1, r - 1 : r - 1 + n, :]
     summed += wr[k, r + 1 : r + 1 + n, :] * u[k + 1, r + 1 : r + 1 + n, :]
-    summed += left * pltpu.roll(here, gap, 1)
-    summed += pltpu.roll(left * here, columns - gap, 1)
-    summed += wv[k, r : r + n, :] * u[k, r : r + n, :]
-    summed += wv[k + 1, r : r + n, :] * u[k + 2, r : r + n, :]
+    if k > 0:
+        summed += wv[k, r : r + n, :] * u[k, r : r + n, :]
+    if k < 5:
+        summed += wv[k + 1, r : r + n, :] * u[k + 2, r : r + n, :]
     return summed
 
 
@@ -229,46 +227,48 @@
     return ((row_of(shape) + lane_of(shape) // gap + k + colour) & 1) == 0
 
 
+def half_sweep(level, source, target, colour, low, high):
+    rhs, coef, wr, wc, wv, gap = level[2:]
+    columns = source.shape[2]
+    for k in range(6):
+        for r, n in spans(low, high, columns):
+            here = source[k + 1, r : r + n, :]
+            new = rhs[k, r : r + n, :] + beside(source, wr, wc, wv, gap, k, r, n, here)
+            new = new * coef[6 + k, r : r + n, :]
+            mask = coloured(n, columns, gap, k, colour)
+            target[k + 1, r : r + n, :] = jnp.where(mask, new, here)
+
+
 def smooth(level, low, high, fresh):
-    u, rhs, coef, wr, wc, wv, gap = level
+    u, v, rhs, coef, wr, wc, wv, gap = level
     columns = u.shape[2]
     if fresh:
-
-        def begin(k, carry):
+        for k in range(6):
             for r, n in spans(low, high, columns):
                 new = rhs[k, r : r + n, :] * coef[6 + k, r : r + n, :]
-                u[k + 1, r : r + n, :] = jnp.where(coloured(n, columns, gap, k, 0), new, 0.0)
-            return carry
-
-        lax.fori_loop(0, 6, begin, 0)
-
-    def half_sweep(step, carry):
-        def layer(k, inner):
-            for r, n in spans(low, high, columns):
-                here = u[k + 1, r : r + n, :]
-                new = rhs[k, r : r + n, :] + beside(u, wr, wc, wv, gap, k, r, n, here)
-                new = new * coef[6 + k, r : r + n, :]
-                u[k + 1, r : r + n, :] = jnp.where(coloured(n, columns, gap, k, step), new, here)
-            return inner
-
-        return lax.fori_loop(0, 6, layer, carry)
-
-    lax.fori_loop(1 if fresh else 0, 4, half_sweep, 0)
+                v[k + 1, r : r + n, :] = jnp.where(coloured(n, columns, gap, k, 0), new, 0.0)
+        half_sweep(level, v, u, 1, low, high)
+        half_sweep(level, u, v, 0, low, high)
+        half_sweep(level, v, u, 1, low, high)
+        return
+
+    def sweep(_, carry):
+        half_sweep(level, u, v, 0, low, high)
+        half_sweep(level, v, u, 1, low, high)
+        return carry
+
+    lax.fori_loop(0, 2, sweep, 0)
 
 
 def residual(level, temp, low, high):
-    u, rhs, coef, wr, wc, wv, gap = level
+    u, _, rhs, coef, wr, wc, wv, gap = level
     columns = u.shape[2]
-
-    def layer(k, carry):
+    for k in range(6):
         for r, n in spans(low, high, columns):
             here = u[k + 1, r : r + n, :]
             left = rhs[k, r : r + n, :] + beside(u, wr, wc, wv, gap, k, r, n, here)
             left = left - coef[12 + k, r : r + n, :] * here
             temp[k, r : r + n, :] = jnp.where(coloured(n, columns, gap, k, 0), left, 0.0)
-        return carry
-
-    lax.fori_loop(0, 6, layer, 0)
 
 
 def left_dot(matrix, values):
@@ -283,7 +283,8 @@
 def pair_rows(ref, i, start, count):
     if ref.shape[2] > LANES:
         shape = (count, 2 * count)
-        return left_dot(chosen(lane_of(shape) // 2 == row_of(shape)), ref[i, start : start + 2 * count, :])
+        pick = chosen(lane_of(shape) // 2 == row_of(shape))
+        return left_dot(pick, ref[i, start : start + 2 * count, :])
     return ref[i, pl.ds(start, count, 2), :] + ref[i, pl.ds(start + 1, count, 2), :]
 
 
@@ -298,14 +299,17 @@
         coarse[i, low_coarse : low_coarse + count, :] = halve(fine, i, low_fine, count, gap)
         return carry
 
-    lax.fori_loop(0, planes, body, 0)
+    if fine.shape[2] > LANES:
+        lax.fori_loop(0, planes, body, 0)
+    else:
+        for i in range(planes):
+            body(i, 0)
 
 
 def prolong(coarse, fine, low, count, to, gap):
     def body(k, carry):
         x = coarse[k + 1, low : low + count, :]
-        if gap:
-            x = x + pltpu.roll(x, gap, 1)
+        x = x + pltpu.roll(x, gap, 1)
         if x.shape[1] > LANES:
             shape = (2 * count, count)
             twice = left_dot(chosen(row_of(shape) // 2 == lane_of(shape)), x)
@@ -315,7 +319,14 @@
         fine[k + 1, pl.ds(to + 1, count, 2), :] += x
         return carry
 
-    lax.fori_loop(0, 6, body, 0)
+    for k in range(6):
+        body(k, 0)
+
+
+def border(ref, planes, pad):
+    rows = ref.shape[1]
+    for start in (0, rows - pad):
+        ref[0:planes, start : start + pad, :] = jnp.zeros((planes, pad, ref.shape[2]), F32)
 
 
 def turned(x, even):
@@ -343,8 +354,7 @@
 
 def build_pair(coef, lab, u, rhs, face, side, low, high):
     half = F32(0.5)
-
-    def faces(k, carry):
+    for k in range(6):
         for r, n in spans(low, high, LANES):
             here = coef[k, r : r + n, :]
             other = coef[6 + k, r : r + n, :]
@@ -353,36 +363,35 @@
             face[12 + k, r : r + n, :] = half * (here + other)
             face[18 + k, r : r + n, :] = half * (here + turned(other, even_of(n, k, 0)))
             v = coef[12 + k, r : r + n, :]
-            below = half * (v + coef[17 + k, r : r + n, :])
-            above = half * (v + coef[19 + k, r : r + n, :])
-            side[k + 1, r : r + n, :] = jnp.where(k > 0, below, 0.0)
-            side[9 + k, r : r + n, :] = jnp.where(k < 5, above, 0.0)
-        return carry
-
-    lax.fori_loop(0, 6, faces, 0)
-
-    def totals(k, carry):
+            if k > 0:
+                side[k + 1, r : r + n, :] = half * (v + coef[17 + k, r : r + n, :])
+            if k < 5:
+                side[9 + k, r : r + n, :] = half * (v + coef[19 + k, r : r + n, :])
+    for k in range(6):
         for r, n in spans(low, high, LANES):
             for colour in (0, 1):
                 s = coef[24 + 6 * colour + k, r : r + n, :]
                 if colour == 0:
                     d = s + face[k, r : r + n, :] + face[6 + k, r : r + n, :]
                     d = d + face[12 + k, r : r + n, :] + face[18 + k, r : r + n, :]
-                    d = d + side[k + 1, r : r + n, :] + side[9 + k, r : r + n, :]
+                    below, above = side[k + 1, r : r + n, :], side[9 + k, r : r + n, :]
                 else:
                     d = s + face[6 + k, r - 1 : r - 1 + n, :] + face[k, r + 1 : r + 1 + n, :]
                     d = d + face[12 + k, r : r + n, :]
                     d = d + turned(face[18 + k, r : r + n, :], even_of(n, k, 1))
-                    d = d + side[8 + k, r : r + n, :] + side[k + 2, r : r + n, :]
-                heat = jnp.where(k == 0, lab[12, r : r + n, :], 0.0)
-                rhs[6 * colour + k, r : r + n, :] = s * u[8 * colour + k + 1, r : r + n, :] + heat
+                    below, above = side[8 + k, r : r + n, :], side[k + 2, r : r + n, :]
+                if k > 0:
+                    d = d + below
+                if k < 5:
+                    d = d + above
+                source = s * u[8 * colour + k + 1, r : r + n, :]
+                if k == 0:
+                    source = source + lab[12, r : r + n, :]
+                rhs[6 * colour + k, r : r + n, :] = source
                 coef[24 + 6 * colour + k, r : r + n, :] = d
                 coef[12 + 6 * colour + k, r : r + n, :] = jnp.where(
                     s > 0.0, F32(1.0) / jnp.where(s > 0.0, d, 1.0), 0.0
                 )
-        return carry
-
-    lax.fori_loop(0, 6, totals, 0)
 
 
 def beside_pair(u, face, side, colour, k, r, n):
@@ -391,47 +400,43 @@
     before = u[o + k + 1, r - 1 : r - 1 + n, :]
     after = u[o + k + 1, r + 1 : r + 1 + n, :]
     even = even_of(n, k, colour)
-    summed = face[12 + k, r : r + n, :] * same
     if colour == 0:
+        summed = face[18 + k, r : r + n, :] * turned(same, even)
+        summed += face[12 + k, r : r + n, :] * same
         summed += face[k, r : r + n, :] * before + face[6 + k, r : r + n, :] * after
-        summed += face[18 + k, r : r + n, :] * turned(same, even)
-        summed += side[k + 1, r : r + n, :] * u[o + k, r : r + n, :]
-        summed += side[9 + k, r : r + n, :] * u[o + k + 2, r : r + n, :]
+        below, above = k + 1, k + 9
     else:
+        summed = turned(face[18 + k, r : r + n, :] * same, even)
+        summed += face[12 + k, r : r + n, :] * same
         summed += face[6 + k, r - 1 : r - 1 + n, :] * before
         summed += face[k, r + 1 : r + 1 + n, :] * after
-        summed += turned(face[18 + k, r : r + n, :] * same, even)
-        summed += side[8 + k, r : r + n, :] * u[o + k, r : r + n, :]
-        summed += side[k + 2, r : r + n, :] * u[o + k + 2, r : r + n, :]
+        below, above = k + 8, k + 2
+    if k > 0:
+        summed += side[below, r : r + n, :] * u[o + k, r : r + n, :]
+    if k < 5:
+        summed += side[above, r : r + n, :] * u[o + k + 2, r : r + n, :]
     return summed
 
 
 def smooth_pair(u, rhs, coef, face, side, low, high):
     def sweep(_, carry):
         for colour in (0, 1):
-
-            def layer(k, inner):
+            for k in range(6):
                 for r, n in spans(low, high, LANES):
                     new = rhs[6 * colour + k, r : r + n, :]
                     new = new + beside_pair(u, face, side, colour, k, r, n)
                     new = new * coef[12 + 6 * colour + k, r : r + n, :]
                     u[8 * colour + k + 1, r : r + n, :] = new
-                return inner
-
-            carry = lax.fori_loop(0, 6, layer, carry)
         return carry
 
     lax.fori_loop(0, 2, sweep, 0)
 
 
 def residual_pair(u, rhs, coef, face, side, temp, low, high):
-    def layer(k, carry):
+    for k in range(6):
         for r, n in spans(low, high, LANES):
             left = rhs[k, r : r + n, :] + beside_pair(u, face, side, 0, k, r, n)
             temp[k, r : r + n, :] = left - coef[24 + k, r : r + n, :] * u[k + 1, r : r + n, :]
-        return carry
-
-    lax.fori_loop(0, 6, layer, 0)
 
 
 def greet(waiting):
@@ -523,7 +528,7 @@
 
 
 def conjugate(level, temp, out):
-    u, rhs, coef, wr, wc, wv, gap = level
+    u, _, rhs, coef, wr, wc, wv, gap = level
     n, columns = u.shape[1] - 16, u.shape[2]
     mid = slice(8, 8 + n)
 
@@ -581,7 +586,7 @@
     shapes = [planes(n, rows) for n in (16, 13, 36, 12, 24, 16, 12)]
     for i in (1, 2):
         r = (n0 >> i) + 2 * BASE
-        shapes += [planes(n, r) for n in (8, 6, 18, 6, 6, 7)]
+        shapes += [planes(n, r) for n in (8, 8, 6, 18, 6, 6, 7)]
     h = n0 >> LOCAL
     shapes += [pltpu.VMEM((ny, nx, 3 * h, LANES), F32), pltpu.VMEM((ny, nx, h, LANES), F32)]
     shapes += [pltpu.SemaphoreType.DMA((nx,)), pltpu.SemaphoreType.DMA((nx,))] * 2
@@ -589,7 +594,7 @@
     columns = up_to(ny * h, LANES)
     for i in range(LEVELS - LOCAL + 1):
         r = ((nx * h) >> i) + 16
-        shapes += [planes(n, r, columns) for n in (8, 6, 18, 6, 6, 7)]
+        shapes += [planes(n, r, columns) for n in (8, 8, 6, 18, 6, 6, 7)]
     shapes += [planes(6, (nx * h) + 16, columns)]
     return shapes
 
@@ -602,16 +607,14 @@
     levels = {}
     at = 7
     for i in (1, 2):
-        u, rhs, coef, wr, wc, wv = refs[at : at + 6]
-        levels[i] = (u, rhs, coef, wr, wc, wv, i)
-        at += 6
+        levels[i] = tuple(refs[at : at + 7]) + (i,)
+        at += 7
     gathered_coef, gathered_rhs = refs[at : at + 2]
     sems = refs[at + 2 : at + 10]
     at += 10
     for i in range(LOCAL, LEVELS + 1):
-        u, rhs, coef, wr, wc, wv = refs[at : at + 6]
-        levels[i] = (u, rhs, coef, wr, wc, wv, 1 << (i - LOCAL))
-        at += 6
+        levels[i] = tuple(refs[at : at + 7]) + (1 << (i - LOCAL),)
+        at += 7
     temp3 = refs[at]
     rest = refs[at + 1 :]
     ex = exchanges(n0)
@@ -619,11 +622,12 @@
         rest = e.bind(rest)
         e.clear()
     greet(False)
-    for ref in (u0, lab, coef0, rhs0, face, side):
-        ref[...] = jnp.zeros_like(ref)
-    for level in levels.values():
-        for ref in level[:6]:
-            ref[...] = jnp.zeros_like(ref)
+    for ref, planes in ((u0, 16), (coef0, 12), (face, 24)):
+        border(ref, planes, BASE - HALO)
+    for i, level in levels.items():
+        pad = BASE - HALO if i < LOCAL else 8
+        for ref, planes in ((level[0], 8), (level[1], 8), (level[3], 6)):
+            border(ref, planes, pad)
 
     r = lax.broadcasted_iota(jnp.int32, (n0, 2 * LANES), 0)
     c = lax.broadcasted_iota(jnp.int32, (n0, 2 * LANES), 1)
@@ -669,15 +673,15 @@
 
     tables = (lat_t, ver_t, sto_t)
     look(lab, coef0, tables, BASE, BASE + n0)
-    coef1, coef2 = levels[1][2], levels[2][2]
-
-    def first(i, carry):
+    coef1, coef2 = levels[1][3], levels[2][3]
+
+    def first(i):
         t, k = i // 6, i % 6
         x = pair_rows(coef0, 12 * t + k, BASE, n1) + pair_rows(coef0, 12 * t + 6 + k, BASE, n1)
         coef1[i, BASE : BASE + n1, :] = x * F32(0.25)
-        return carry
-
-    lax.fori_loop(0, 18, first, 0)
+
+    for i in range(18):
+        first(i)
     restrict(coef1, coef2, 18, BASE, BASE, n2, 1)
     ex["coef1"].start([(coef1, (i,)) for i in range(18)], (coef1,))
     ex["coef2"].start([(coef2, (i,)) for i in range(18)], (coef2,))
@@ -697,13 +701,10 @@
     smooth_pair(u0, rhs0, coef0, face, side, lo, hi0)
     temp = coef0
     residual_pair(u0, rhs0, coef0, face, side, temp, BASE, BASE + n0)
-    rhs1, rhs2 = levels[1][1], levels[2][1]
-
-    def down(k, carry):
+    rhs1, rhs2 = levels[1][2], levels[2][2]
+
+    for k in range(6):
         rhs1[k, BASE : BASE + n1, :] = pair_rows(temp, k, BASE, n1) * F32(0.25)
-        return carry
-
-    lax.fori_loop(0, 6, down, 0)
     ex["rhs1"].start([(rhs1, (k,)) for k in range(6)], (rhs1,))
     for c in (0, 1):
         stage[6 * c : 6 * c + 6, own, :] = u0[1 + 8 * c : 7 + 8 * c, own, :]
@@ -716,7 +717,7 @@
         e.unpack(planes, [(e.tops[0], i) for i in range(count)], planes)
 
     def weigh(i, low, high):
-        u, rhs, coef, wr, wc, wv, gap = levels[i]
+        coef, wr, wc, wv, gap = levels[i][3:]
         build(coef, wr, wc, wv, 0.25**i, gap, low, high)
 
     fill("coef1", coef1, 18)
@@ -735,7 +736,7 @@
     ex["rhs2"].start([(rhs2, (k,)) for k in range(6)], (rhs2,))
     ex["u1"].start([(u1, (k + 1,)) for k in range(6)], (u1.at[1:7],))
     end(coef_y)
-    coef3 = levels[3][2]
+    coef3 = levels[3][3]
     place(gathered_coef, [(coef3, 0), (coef3, 6), (coef3, 12)], h)
 
     fill("rhs2", rhs2, 6)
@@ -749,22 +750,22 @@
 
     sizes = {i: (nx * h) >> (i - LOCAL) for i in range(LOCAL, LEVELS + 1)}
     for i in range(LOCAL, LEVELS):
-        restrict(levels[i][2], levels[i + 1][2], 18, 8, 8, sizes[i + 1], levels[i][6])
+        restrict(levels[i][3], levels[i + 1][3], 18, 8, 8, sizes[i + 1], levels[i][-1])
     end(rhs_x)
     rhs_y = gather_copies(gathered_rhs, sems[6:8], "gy")
     begin(rhs_y)
     for i in range(LOCAL, LEVELS + 1):
         weigh(i, 8, 8 + sizes[i])
     end(rhs_y)
-    place(gathered_rhs, [(levels[3][1], 0)], h)
+    place(gathered_rhs, [(levels[3][2], 0)], h)
 
     for i in range(LOCAL, LEVELS):
         smooth(levels[i], 8, 8 + sizes[i], True)
         residual(levels[i], temp3, 8, 8 + sizes[i])
-        restrict(temp3, levels[i + 1][1], 6, 8, 8, sizes[i + 1], levels[i][6])
-    conjugate(levels[LEVELS], temp3, levels[LEVELS][1])
+        restrict(temp3, levels[i + 1][2], 6, 8, 8, sizes[i + 1], levels[i][-1])
+    conjugate(levels[LEVELS], temp3, levels[LEVELS][2])
     for i in reversed(range(LOCAL, LEVELS)):
-        prolong(levels[i + 1][0], levels[i][0], 8, sizes[i + 1], 8, levels[i][6])
+        prolong(levels[i + 1][0], levels[i][0], 8, sizes[i + 1], 8, levels[i][-1])
         smooth(levels[i], 8, 8 + sizes[i], False)
 
     u3 = levels[3][0]
@@ -775,14 +776,11 @@
     widen = chosen(hit)
     fill("u2", u2, 6, 1)
 
-    def window(k, carry):
+    for k in range(6):
         x = u3[k + 1, pl.ds(pl.multiple_of(gx * h, 8), h + 16), :]
         x = split_dot(x, widen)
         u2[k + 1, pl.ds(0, h + 16, 2), :] += x
         u2[k + 1, pl.ds(1, h + 16, 2), :] += x
-        return carry
-
-    lax.fori_loop(0, 6, window, 0)
     smooth(levels[2], lo, hi2, False)
     fill("u1", u1, 6, 1)
     prolong(u2, u1, lo, n2 + 16, 0, 1)
@@ -791,14 +789,11 @@
     e.finish()
     e.unpack(fields, [(e.tops[0], i) for i in range(12)], fields)
 
-    def up(k, carry):
+    for k in range(6):
         x = u1[k + 1, lo : lo + n1 + 16, :]
         for c in (0, 8):
             u0[c + k + 1, pl.ds(0, n1 + 16, 2), :] += x
             u0[c + k + 1, pl.ds(1, n1 + 16, 2), :] += x
-        return carry
-
-    lax.fori_loop(0, 6, up, 0)
     smooth_pair(u0, rhs0, coef0, face, side, lo, hi0)
 
     r = lax.broadcasted_iota(jnp.int32, (2 * LANES, n0), 0)

time: 85.7 us -> 62.4 us (0.73)
  Pallas kernels: 83.7 us -> 60.5 us
    pallas_call x1, Pallas kernels: 83.7 us -> 60.5 us  [on_device(): pl.pallas_call(whole_kernel, out_shape=jax.ShapeDtypeStruct(field.shape,...]
where the time goes in v3:
time: 62.4 us; the launch traced here: 62.2 us
  Pallas kernels  60.5 us (97%)
  local copies, waits for them, and re-layouts  1.77 us (3%)
    pallas_call x1, Pallas kernels, on_device(): pl.pallas_call(whole_kernel, out_shape=jax.ShapeDtypeStruct(field.shape,...  60.5 us
    unnamed x1, local copies, waits for them, and re-layouts  1.77 us

profile of v3, /device:TPU:0, one launch (start us, length us, event | category | flops | bytes accessed | tf_op | source)
XLA Modules:
  0.0 62.2 jit_solution(15676348849948901233)
XLA Ops:
  0.0 60.5 %shard_map.73 = f32[6,128,128]{2,1,0:T(8,128)} custom-call(f32[6,128,128]{2,1,0:T(8,128)} %field.1, s32[6,128,128]{2,1,0:T(8,128)} %labels.1, s32[8,8]{1,0:T(8,128)} %patch.1, f32[8]{0:T(128)} %lat_t.1, f32[8]{0:T(128)} %ver_t.1, f32[8]{0:T(128)} %sto_t.1, f32[64]{0:T(128)} %wattage.1), custom_call_target="tpu_custom_call" | custom-call | tf_op jit(solution)/shard_map/pallas_call | solution.py:823
  60.5 1.8 %copy.9 = f32[6,128,128]{2,1,0:T(8,128)} copy(f32[6,128,128]{2,1,0:T(8,128)} %shard_map.73) | data formatting | bytes 786432

commit v4 on v3

--- a/solution.py
+++ b/solution.py
@@ -67,16 +67,24 @@
 
 
 class Exchange:
-    def __init__(self, width, rows, count, row_refs):
-        self.width, self.rows, self.count = width, rows, count
-        self.per = LANES // width
-        self.packs = -(-count // self.per)
-        self.row_refs = row_refs
+    def __init__(self, rows, groups, row_refs):
+        self.rows, self.row_refs = rows, row_refs
+        self.twin = [g[2] for g in groups]
+        self.slots, pack, lane = [], 0, 0
+        for width, count, _ in groups:
+            group = []
+            for _ in range(count):
+                if lane + width > LANES:
+                    pack, lane = pack + 1, 0
+                group.append((pack, lane, width))
+                lane += width
+            self.slots.append(group)
+        self.packs = pack + 1
 
     def scratch(self):
         packed = pltpu.VMEM((2, self.packs, self.rows, LANES), F32)
         landed = pltpu.VMEM((2, self.packs, self.rows + 2 * HALO, LANES), F32)
-        tops = [pltpu.VMEM((2, n, HALO, LANES), F32) for n in self.row_refs]
+        tops = [pltpu.VMEM((2, n, HALO, LANES), F32) for n, _ in self.row_refs]
         sems = pltpu.SemaphoreType.DMA((6 + 2 * len(self.row_refs),))
         return [packed, landed, sems, sems] + tops
 
@@ -90,28 +98,23 @@
         for top in self.tops:
             top[...] = jnp.zeros_like(top)
 
-    def copies(self, sources):
+    def copies(self):
         n = self.rows
         gx, gy = lax.axis_index("gx"), lax.axis_index("gy")
         out = []
-        at = 0
-
-        def add(dx, dy, source, target):
-            nonlocal at
-            out.append((dx, dy, source, target, at))
-            at += 1
-
         for dy, side in ((1, 0), (-1, 1)):
             packed = self.packed.at[side]
             landed = self.landed.at[side]
-            add(0, dy, packed, landed.at[:, HALO : HALO + n, :])
-            add(1, dy, packed.at[:, n - HALO : n, :], landed.at[:, 0:HALO, :])
-            add(-1, dy, packed.at[:, 0:HALO, :], landed.at[:, HALO + n : n + 2 * HALO, :])
-        for source, top in zip(sources, self.tops):
-            add(1, 0, source.at[:, BASE + n - HALO : BASE + n, :], top.at[0])
-            add(-1, 0, source.at[:, BASE : BASE + HALO, :], top.at[1])
+            out.append((0, dy, packed, landed.at[:, HALO : HALO + n, :]))
+            out.append((1, dy, packed.at[:, n - HALO : n, :], landed.at[:, 0:HALO, :]))
+            out.append(
+                (-1, dy, packed.at[:, 0:HALO, :], landed.at[:, HALO + n : n + 2 * HALO, :])
+            )
+        for source, top, (_, m) in zip(self.sources, self.tops, self.row_refs):
+            out.append((1, 0, source.at[:, BASE + m - HALO : BASE + m, :], top.at[0]))
+            out.append((-1, 0, source.at[:, BASE : BASE + HALO, :], top.at[1]))
         made = []
-        for dx, dy, source, target, i in out:
+        for i, (dx, dy, source, target) in enumerate(out):
             copy = pltpu.make_async_remote_copy(
                 src_ref=source,
                 dst_ref=target,
@@ -123,54 +126,86 @@
             made.append((dx, dy, copy))
         return made
 
-    def start(self, planes, sources):
-        w = self.width
-        n = self.rows
-        for pack in range(self.packs):
-            group = planes[pack * self.per : (pack + 1) * self.per]
-            for r, m in spans(0, n, LANES):
-                lane = lane_of((m, LANES)) // w
-                right = jnp.zeros((m, LANES), F32)
-                left = right
-                for p, (ref, where) in enumerate(group):
-                    x = ref[where + (slice(BASE + r, BASE + r + m),)]
-                    hit = lane == p
-                    a = pltpu.roll(x, (p * w - (LEFT + 64 - w)) % LANES, 1)
-                    b = pltpu.roll(x, (p * w - LEFT) % LANES, 1)
-                    right = jnp.where(hit, a, right)
-                    left = jnp.where(hit, b, left)
-                self.packed[0, pack, r : r + m, :] = right
-                self.packed[1, pack, r : r + m, :] = left
+    def start(self, groups, sources):
+        slots = [x for group in self.slots for x in group]
+        takes = [x for group in groups for x in group]
+        for r, m in spans(0, self.rows, LANES):
+            lane = lane_of((m, LANES))
+            packs = [[jnp.zeros((m, LANES), F32)] * 2 for _ in range(self.packs)]
+            for (pack, at, w), take in zip(slots, takes):
+                x = take(r, m)
+                hit = (lane >= at) & (lane < at + w)
+                a = pltpu.roll(x, (at - (LEFT + 64 - w)) % LANES, 1)
+                b = pltpu.roll(x, (at - LEFT) % LANES, 1)
+                right, left = packs[pack]
+                packs[pack] = [jnp.where(hit, a, right), jnp.where(hit, b, left)]
+            for pack, both in enumerate(packs):
+                for side in (0, 1):
+                    self.packed[side, pack, r : r + m, :] = both[side]
         self.sources = sources
-        for dx, dy, copy in self.copies(sources):
+        for dx, dy, copy in self.copies():
             pl.when(near(dx, dy))(copy.start)
 
     def finish(self):
-        for dx, dy, copy in self.copies(self.sources):
+        for dx, dy, copy in self.copies():
             pl.when(near(dx, dy))(copy.wait_send)
             pl.when(near(-dx, -dy))(copy.wait_recv)
 
-    def unpack(self, planes, tops, targets):
-        w = self.width
+    def merge(self, x, slot, r, m, shift=None):
+        pack, at, w = slot
+        lane = lane_of((m, LANES))
+        inside = (lane >= LEFT - w) & (lane < LEFT)
+        beyond = (lane >= LEFT + 64) & (lane < LEFT + 64 + w)
+        if shift is not None:
+            inside, beyond = inside & (lane % 2 == 0), beyond & (lane % 2 == 0)
+        back = shift or 0
+        a = pltpu.roll(self.landed[0, pack, r : r + m, :], (LEFT - w - at - back) % LANES, 1)
+        b = pltpu.roll(self.landed[1, pack, r : r + m, :], (LEFT + 64 - at - back) % LANES, 1)
+        return jnp.where(beyond, b, jnp.where(inside, a, x))
+
+    def unpack(self, group, planes, tops):
         n = self.rows
-        for i, (ref, where) in enumerate(planes):
-            pack, p = i // self.per, i % self.per
-            target, place = targets[i]
+        for i, (ref, plane) in enumerate(planes):
+            twin = self.twin[group]
+            slot = self.slots[group][i // 2 if twin else i]
             pieces = [(0, HALO, 0)]
             pieces += [(HALO + r, m, None) for r, m in spans(0, n, LANES)]
             pieces += [(HALO + n, HALO, 1)]
             for r, m, side in pieces:
+                rows = slice(BASE - HALO + r, BASE - HALO + r + m)
                 if side is None:
-                    x = ref[where + (slice(BASE - HALO + r, BASE - HALO + r + m),)]
+                    x = ref[plane, rows]
                 else:
-                    top, plane = tops[i]
-                    x = top[side, plane]
-                lane = lane_of((m, LANES))
-                a = pltpu.roll(self.landed[0, pack, r : r + m, :], (LEFT - w - p * w) % LANES, 1)
-                b = pltpu.roll(self.landed[1, pack, r : r + m, :], (LEFT + 64 - p * w) % LANES, 1)
-                x = jnp.where((lane >= LEFT - w) & (lane < LEFT), a, x)
-                x = jnp.where((lane >= LEFT + 64) & (lane < LEFT + 64 + w), b, x)
-                target[place + (slice(BASE - HALO + r, BASE - HALO + r + m),)] = x
+                    x = tops[i][0][side, tops[i][1]]
+                ref[plane, rows] = self.merge(x, slot, r, m, i % 2 if twin else None)
+
+    def unpack_folded(self, group, planes, tops):
+        n = self.rows
+        for i, (ref, plane) in enumerate(planes):
+            top, at = tops[i]
+            ref[plane, BASE - HALO : BASE] = top[0, at]
+            ref[plane, BASE + 2 * n : BASE + 2 * n + HALO] = top[1, at]
+            for odd in (0, 1):
+                for r, m in spans(HALO // 2, n + HALO + HALO // 2, LANES):
+                    rows = pl.ds(BASE + 2 * (r - HALO) + odd, m, 2)
+                    slot = self.slots[group][2 * i + odd]
+                    ref[plane, rows, :] = self.merge(ref[plane, rows, :], slot, r, m)
+
+
+def rows_of(ref, plane):
+    return lambda r, m: ref[plane, BASE + r : BASE + r + m, :]
+
+
+def twins_of(ref, plane):
+    def take(r, m):
+        a, b = ref[plane, BASE + r : BASE + r + m, :], ref[plane + 1, BASE + r : BASE + r + m, :]
+        return jnp.where(lane_of(a.shape) % 2 == 0, a, pltpu.roll(b, 1, 1))
+
+    return take
+
+
+def folds_of(ref, plane, odd):
+    return lambda r, m: ref[plane, pl.ds(BASE + odd + 2 * r, m, 2), :]
 
 
 def build(coef, wr, wc, wv, scale, gap, low, high):
@@ -462,28 +497,35 @@
             pl.semaphore_signal(barrier, inc=1, device_id=other, device_id_type=MESH)
 
 
-def gather_copies(whole, sems, axis):
-    size = lax.axis_size(axis)
+def gather_copies(whole, sems, phase):
+    nx, ny = lax.axis_size("gx"), lax.axis_size("gy")
     gx, gy = lax.axis_index("gx"), lax.axis_index("gy")
+    half = nx // 2
+    kind, at = lax.rem(gx, 2), gx // 2
+    moves = []
+    if phase == 0:
+        for step in range(1, half):
+            target = (2 * lax.rem(at + step, half) + kind, gy)
+            origin = lax.rem(at + half - step, half)
+            moves.append((target, whole.at[kind, gy, at], whole.at[kind, gy, origin]))
+    elif phase == 1:
+        for step in range(1, ny):
+            target = (gx, lax.rem(gy + step, ny))
+            origin = lax.rem(gy + ny - step, ny)
+            moves.append((target, whole.at[kind, gy], whole.at[kind, origin]))
+    else:
+        moves.append(((gx + 1 - 2 * kind, gy), whole.at[kind], whole.at[1 - kind]))
     made = []
-    for step in range(1, size):
-        if axis == "gx":
-            target = (lax.rem(gx + step, size), gy)
-            source = whole.at[gy, gx]
-            origin = whole.at[gy, lax.rem(gx + size - step, size)]
-        else:
-            target = (gx, lax.rem(gy + step, size))
-            source = whole.at[gy]
-            origin = whole.at[lax.rem(gy + size - step, size)]
-        out = pltpu.make_async_remote_copy(
-            src_ref=source, dst_ref=source, send_sem=sems[0].at[step],
-            recv_sem=sems[1].at[step], device_id=target, device_id_type=MESH,
-        )
-        into = pltpu.make_async_remote_copy(
-            src_ref=origin, dst_ref=origin, send_sem=sems[0].at[step],
-            recv_sem=sems[1].at[step], device_id=target, device_id_type=MESH,
-        )
-        made.append((out, into))
+    for i, (target, source, arriving) in enumerate(moves):
+        both = []
+        for ref in (source, arriving):
+            both.append(
+                pltpu.make_async_remote_copy(
+                    src_ref=ref, dst_ref=ref, send_sem=sems[2 * phase].at[i],
+                    recv_sem=sems[2 * phase + 1].at[i], device_id=target, device_id_type=MESH,
+                )
+            )
+        made.append(both)
     return made
 
 
@@ -507,24 +549,25 @@
 
 
 def place(whole, targets, h):
-    ny, nx = whole.shape[:2]
+    _, ny, half = whole.shape[:3]
     wide = min(ny, LANES // 16)
 
-    def body(gx, carry):
-        row = pl.multiple_of(8 + gx * h, 8)
-        for t, (ref, first) in enumerate(targets):
-            for k in range(6):
-                for start in range(0, ny, wide):
-                    total = jnp.zeros((h, LANES), F32)
-                    lane = lane_of((h, LANES)) // 16
-                    for gy in range(start, min(start + wide, ny)):
-                        x = whole[gy, gx, t * h : (t + 1) * h, :]
-                        x = pltpu.roll(x, (16 * (gy - start - k)) % LANES, 1)
-                        total = jnp.where(lane == gy - start, x, total)
-                    ref[first + k, pl.ds(row, h), start * 16 : start * 16 + LANES] = total
+    def body(at, carry):
+        lane = lane_of((h, LANES)) // 16
+        for kind in (0, 1):
+            row = pl.multiple_of(8 + (2 * at + kind) * h, 8)
+            for t, (ref, first) in enumerate(targets):
+                for k in range(6):
+                    for start in range(0, ny, wide):
+                        total = jnp.zeros((h, LANES), F32)
+                        for gy in range(start, min(start + wide, ny)):
+                            x = whole[kind, gy, at, t * h : (t + 1) * h, :]
+                            x = pltpu.roll(x, (16 * (gy - start - k)) % LANES, 1)
+                            total = jnp.where(lane == gy - start, x, total)
+                        ref[first + k, pl.ds(row, h), start * 16 : start * 16 + LANES] = total
         return carry
 
-    lax.fori_loop(0, nx, body, 0)
+    lax.fori_loop(0, half, body, 0)
 
 
 def conjugate(level, temp, out):
@@ -567,14 +610,12 @@
 def exchanges(n0):
     n1, n2 = n0 // 2, n0 // 4
     return {
-        "near": Exchange(4, n0, 25, (12, 13)),
-        "coef1": Exchange(8, n1, 18, (18,)),
-        "coef2": Exchange(16, n2, 18, (18,)),
-        "u0": Exchange(4, n0, 12, (12,)),
-        "rhs1": Exchange(8, n1, 6, (6,)),
-        "u1": Exchange(8, n1, 6, (6,)),
-        "rhs2": Exchange(16, n2, 6, (6,)),
-        "u2": Exchange(16, n2, 6, (6,)),
+        "near": Exchange(n0, [(4, 12, False), (4, 13, False)], [(12, n0), (13, n0)]),
+        "coef1": Exchange(n1, [(7, 18, False)], [(18, n1)]),
+        "coef2": Exchange(n2, [(14, 9, True)], [(18, n2)]),
+        "rhs1": Exchange(n1, [(6, 6, False), (2, 24, False)], [(6, n1), (12, n0)]),
+        "rhs2": Exchange(n2, [(12, 3, True), (6, 12, False)], [(6, n2), (6, n1)]),
+        "u2": Exchange(n2, [(14, 3, True)], [(6, n2)]),
     }
 
 
@@ -588,9 +629,11 @@
         r = (n0 >> i) + 2 * BASE
         shapes += [planes(n, r) for n in (8, 8, 6, 18, 6, 6, 7)]
     h = n0 >> LOCAL
-    shapes += [pltpu.VMEM((ny, nx, 3 * h, LANES), F32), pltpu.VMEM((ny, nx, h, LANES), F32)]
-    shapes += [pltpu.SemaphoreType.DMA((nx,)), pltpu.SemaphoreType.DMA((nx,))] * 2
-    shapes += [pltpu.SemaphoreType.DMA((ny,)), pltpu.SemaphoreType.DMA((ny,))] * 2
+    for n in (3 * h, h):
+        shapes += [pltpu.VMEM((2, ny, nx // 2, n, LANES), F32)]
+    for _ in range(2):
+        for n in (nx, nx, ny, ny, 1, 1):
+            shapes += [pltpu.SemaphoreType.DMA((n,))]
     columns = up_to(ny * h, LANES)
     for i in range(LEVELS - LOCAL + 1):
         r = ((nx * h) >> i) + 16
@@ -610,8 +653,8 @@
         levels[i] = tuple(refs[at : at + 7]) + (i,)
         at += 7
     gathered_coef, gathered_rhs = refs[at : at + 2]
-    sems = refs[at + 2 : at + 10]
-    at += 10
+    coef_sems, rhs_sems = refs[at + 2 : at + 8], refs[at + 8 : at + 14]
+    at += 14
     for i in range(LOCAL, LEVELS + 1):
         levels[i] = tuple(refs[at : at + 7]) + (1 << (i - LOCAL),)
         at += 7
@@ -662,14 +705,20 @@
             heat[i : i + 1, :], (TILE, LANES)
         )
 
-    fields = [(u0, (1 + k + 8 * c,)) for c in (0, 1) for k in range(6)]
-    labs = [(lab, (i,)) for i in range(13)]
+    fields = [(u0, 1 + k + 8 * c) for c in (0, 1) for k in range(6)]
+    labs = [(lab, i) for i in range(13)]
     edge = ex["near"]
     stage = lab_own
-    for c in (0, 1):
-        stage[6 * c : 6 * c + 6, own, :] = u0[1 + 8 * c : 7 + 8 * c, own, :]
+
+    def restage():
+        for c in (0, 1):
+            for r in (BASE, BASE + n0 - HALO):
+                rows = slice(r, r + HALO)
+                stage[6 * c : 6 * c + 6, rows, :] = u0[1 + 8 * c : 7 + 8 * c, rows, :]
+
+    restage()
     greet(True)
-    edge.start(fields + labs, (stage, lab))
+    edge.start([[rows_of(*p) for p in fields], [rows_of(*p) for p in labs]], (stage, lab))
 
     tables = (lat_t, ver_t, sto_t)
     look(lab, coef0, tables, BASE, BASE + n0)
@@ -683,21 +732,24 @@
     for i in range(18):
         first(i)
     restrict(coef1, coef2, 18, BASE, BASE, n2, 1)
-    ex["coef1"].start([(coef1, (i,)) for i in range(18)], (coef1,))
-    ex["coef2"].start([(coef2, (i,)) for i in range(18)], (coef2,))
+    ex["coef1"].start([[rows_of(coef1, i) for i in range(18)]], (coef1,))
+    ex["coef2"].start([[twins_of(coef2, i) for i in range(0, 18, 2)]], (coef2,))
     gx, gy = lax.axis_index("gx"), lax.axis_index("gy")
+    mine = (lax.rem(gx, 2), gy, gx // 2)
     for t in range(3):
         planes = [halve(coef2, 6 * t + k, BASE, h, 2) for k in range(6)]
-        gathered_coef[gy, gx, t * h : (t + 1) * h, :] = squeeze(planes)
-    coef_x = gather_copies(gathered_coef, sems[0:2], "gx")
-    begin(coef_x)
+        gathered_coef[mine + (slice(t * h, (t + 1) * h),)] = squeeze(planes)
+    coef_moves = [gather_copies(gathered_coef, coef_sems, phase) for phase in range(3)]
+    begin(coef_moves[0])
 
     edge.finish()
-    tops = [(edge.tops[0], i) for i in range(12)] + [(edge.tops[1], i) for i in range(13)]
-    edge.unpack(fields + labs, tops, fields + labs)
+    edge.unpack(0, fields, [(edge.tops[0], i) for i in range(12)])
+    edge.unpack(1, labs, [(edge.tops[1], i) for i in range(13)])
     lo, hi0, hi1, hi2 = BASE - HALO, BASE + n0 + HALO, BASE + n1 + HALO, BASE + n2 + HALO
     look(lab, coef0, tables, lo, hi0)
     build_pair(coef0, lab, u0, rhs0, face, side, lo, hi0)
+    end(coef_moves[0])
+    begin(coef_moves[1])
     smooth_pair(u0, rhs0, coef0, face, side, lo, hi0)
     temp = coef0
     residual_pair(u0, rhs0, coef0, face, side, temp, BASE, BASE + n0)
@@ -705,16 +757,14 @@
 
     for k in range(6):
         rhs1[k, BASE : BASE + n1, :] = pair_rows(temp, k, BASE, n1) * F32(0.25)
-    ex["rhs1"].start([(rhs1, (k,)) for k in range(6)], (rhs1,))
-    for c in (0, 1):
-        stage[6 * c : 6 * c + 6, own, :] = u0[1 + 8 * c : 7 + 8 * c, own, :]
-    ex["u0"].start(fields, (stage,))
+    restage()
+    folded = [folds_of(ref, plane, odd) for ref, plane in fields for odd in (0, 1)]
+    ex["rhs1"].start([[rows_of(rhs1, k) for k in range(6)], folded], (rhs1, stage))
 
     def fill(name, ref, count, first=0):
         e = ex[name]
         e.finish()
-        planes = [(ref, (first + i,)) for i in range(count)]
-        e.unpack(planes, [(e.tops[0], i) for i in range(count)], planes)
+        e.unpack(0, [(ref, first + i) for i in range(count)], [(e.tops[0], i) for i in range(count)])
 
     def weigh(i, low, high):
         coef, wr, wc, wv, gap = levels[i][3:]
@@ -724,39 +774,39 @@
     weigh(1, lo, hi1)
     fill("coef2", coef2, 18)
     weigh(2, lo, hi2)
-    end(coef_x)
-    coef_y = gather_copies(gathered_coef, sems[4:6], "gy")
-    begin(coef_y)
 
     fill("rhs1", rhs1, 6)
     smooth(levels[1], lo, hi1, True)
     u1 = levels[1][0]
     residual(levels[1], temp, BASE, BASE + n1)
     restrict(temp, rhs2, 6, BASE, BASE, n2, 1)
-    ex["rhs2"].start([(rhs2, (k,)) for k in range(6)], (rhs2,))
-    ex["u1"].start([(u1, (k + 1,)) for k in range(6)], (u1.at[1:7],))
-    end(coef_y)
-    coef3 = levels[3][3]
-    place(gathered_coef, [(coef3, 0), (coef3, 6), (coef3, 12)], h)
+    folded = [folds_of(u1, k + 1, odd) for k in range(6) for odd in (0, 1)]
+    ex["rhs2"].start([[twins_of(rhs2, k) for k in (0, 2, 4)], folded], (rhs2, u1.at[1:7]))
+    end(coef_moves[1])
+    begin(coef_moves[2])
 
     fill("rhs2", rhs2, 6)
     smooth(levels[2], lo, hi2, True)
     u2 = levels[2][0]
     residual(levels[2], temp, BASE, BASE + n2)
-    gathered_rhs[gy, gx] = squeeze([halve(temp, k, BASE, h, 2) for k in range(6)])
-    rhs_x = gather_copies(gathered_rhs, sems[2:4], "gx")
-    begin(rhs_x)
-    ex["u2"].start([(u2, (k + 1,)) for k in range(6)], (u2.at[1:7],))
+    gathered_rhs[mine] = squeeze([halve(temp, k, BASE, h, 2) for k in range(6)])
+    rhs_moves = [gather_copies(gathered_rhs, rhs_sems, phase) for phase in range(3)]
+    begin(rhs_moves[0])
+    ex["u2"].start([[twins_of(u2, k) for k in (1, 3, 5)]], (u2.at[1:7],))
+    end(coef_moves[2])
+    coef3 = levels[3][3]
+    place(gathered_coef, [(coef3, 0), (coef3, 6), (coef3, 12)], h)
 
     sizes = {i: (nx * h) >> (i - LOCAL) for i in range(LOCAL, LEVELS + 1)}
     for i in range(LOCAL, LEVELS):
         restrict(levels[i][3], levels[i + 1][3], 18, 8, 8, sizes[i + 1], levels[i][-1])
-    end(rhs_x)
-    rhs_y = gather_copies(gathered_rhs, sems[6:8], "gy")
-    begin(rhs_y)
+    end(rhs_moves[0])
+    begin(rhs_moves[1])
     for i in range(LOCAL, LEVELS + 1):
         weigh(i, 8, 8 + sizes[i])
-    end(rhs_y)
+    end(rhs_moves[1])
+    begin(rhs_moves[2])
+    end(rhs_moves[2])
     place(gathered_rhs, [(levels[3][2], 0)], h)
 
     for i in range(LOCAL, LEVELS):
@@ -782,12 +832,12 @@
         u2[k + 1, pl.ds(0, h + 16, 2), :] += x
         u2[k + 1, pl.ds(1, h + 16, 2), :] += x
     smooth(levels[2], lo, hi2, False)
-    fill("u1", u1, 6, 1)
+    e = ex["rhs2"]
+    e.unpack_folded(1, [(u1, k + 1) for k in range(6)], [(e.tops[1], k) for k in range(6)])
     prolong(u2, u1, lo, n2 + 16, 0, 1)
     smooth(levels[1], lo, hi1, False)
-    e = ex["u0"]
-    e.finish()
-    e.unpack(fields, [(e.tops[0], i) for i in range(12)], fields)
+    e = ex["rhs1"]
+    e.unpack_folded(1, fields, [(e.tops[1], i) for i in range(12)])
 
     for k in range(6):
         x = u1[k + 1, lo : lo + n1 + 16, :]

time: 62.4 us -> 55.6 us (0.89)
  Pallas kernels: 60.5 us -> 53.7 us
    pallas_call x1, Pallas kernels: 60.5 us -> 53.7 us  [on_device(): pl.pallas_call(whole_kernel, out_shape=jax.ShapeDtypeStruct(field.shape,...]
where the time goes in v4:
time: 55.6 us; the launch traced here: 55.4 us
  Pallas kernels  53.7 us (97%)
  local copies, waits for them, and re-layouts  1.77 us (3%)
    pallas_call x1, Pallas kernels, on_device(): pl.pallas_call(whole_kernel, out_shape=jax.ShapeDtypeStruct(field.shape,...  53.7 us
    unnamed x1, local copies, waits for them, and re-layouts  1.77 us

profile of v4, /device:TPU:0, one launch (start us, length us, event | category | flops | bytes accessed | tf_op | source)
XLA Modules:
  0.0 55.4 jit_solution(16197891103776110058)
XLA Ops:
  0.0 53.7 %shard_map.73 = f32[6,128,128]{2,1,0:T(8,128)} custom-call(f32[6,128,128]{2,1,0:T(8,128)} %field.1, s32[6,128,128]{2,1,0:T(8,128)} %labels.1, s32[8,8]{1,0:T(8,128)} %patch.1, f32[8]{0:T(128)} %lat_t.1, f32[8]{0:T(128)} %ver_t.1, f32[8]{0:T(128)} %sto_t.1, f32[64]{0:T(128)} %wattage.1), custom_call_target="tpu_custom_call" | custom-call | tf_op jit(solution)/shard_map/pallas_call | solution.py:873
  53.7 1.8 %copy.9 = f32[6,128,128]{2,1,0:T(8,128)} copy(f32[6,128,128]{2,1,0:T(8,128)} %shard_map.73) | data formatting | bytes 786432

commit v5 on v4

--- a/solution.py
+++ b/solution.py
@@ -126,7 +126,7 @@
             made.append((dx, dy, copy))
         return made
 
-    def start(self, groups, sources):
+    def start(self, groups, sources, now=True):
         slots = [x for group in self.slots for x in group]
         takes = [x for group in groups for x in group]
         for r, m in spans(0, self.rows, LANES):
@@ -143,6 +143,10 @@
                 for side in (0, 1):
                     self.packed[side, pack, r : r + m, :] = both[side]
         self.sources = sources
+        if now:
+            self.launch()
+
+    def launch(self):
         for dx, dy, copy in self.copies():
             pl.when(near(dx, dy))(copy.start)
 
@@ -570,41 +574,51 @@
     lax.fori_loop(0, half, body, 0)
 
 
-def conjugate(level, temp, out):
-    u, _, rhs, coef, wr, wc, wv, gap = level
-    n, columns = u.shape[1] - 16, u.shape[2]
+def conjugate(level, residue):
+    u, v, rhs, coef, wr, wc, wv, gap = level
+    n = u.shape[1] - 16
     mid = slice(8, 8 + n)
 
     def summed(x):
-        x = jnp.sum(x, axis=0)
-        return jnp.sum(jnp.sum(x, axis=0, keepdims=True), axis=1, keepdims=True)
-
-    inv = slice(6, 12)
-    r0 = rhs[:, mid, :]
-    z0 = r0 * coef[inv, mid, :]
-    u[1:7, mid, :] = z0
-    temp[:, mid, :] = r0
-    out[:, mid, :] = jnp.zeros_like(r0)
-
-    def step(_, rz):
-        p = u[1:7, mid, :]
-        image = jnp.stack(
-            [
-                coef[12 + k, mid, :] * p[k] - beside(u, wr, wc, wv, gap, k, 8, n, p[k])
-                for k in range(6)
-            ]
-        )
-        alpha = rz / summed(p * image)
-        out[:, mid, :] += alpha[None] * p
-        r = temp[:, mid, :] - alpha[None] * image
-        temp[:, mid, :] = r
-        z = r * coef[inv, mid, :]
-        rz_new = summed(r * z)
-        u[1:7, mid, :] = z + (rz_new / rz)[None] * p
-        return rz_new
-
-    lax.fori_loop(0, COARSE_ITERS, step, summed(r0 * z0))
-    u[1:7, mid, :] = out[:, mid, :]
+        total = (x[0] + x[1]) + (x[2] + x[3]) + (x[4] + x[5])
+        return jnp.sum(jnp.sum(total, axis=0, keepdims=True), axis=1, keepdims=True)
+
+    def turn(r):
+        z = [r[k] * coef[6 + k, mid, :] for k in range(6)]
+        for k in range(6):
+            u[k + 1, mid, :] = z[k]
+        w = [
+            coef[12 + k, mid, :] * z[k] - beside(u, wr, wc, wv, gap, k, 8, n, z[k])
+            for k in range(6)
+        ]
+        rz = summed([a * b for a, b in zip(r, z)])
+        return z, w, rz, summed([a * b for a, b in zip(w, z)])
+
+    r = [rhs[k, mid, :] for k in range(6)]
+    z, w, rz, zaz = turn(r)
+    for k in range(6):
+        residue[k, mid, :] = r[k]
+        v[k + 1, mid, :] = z[k]
+        coef[k, mid, :] = w[k]
+        rhs[k, mid, :] = jnp.zeros_like(r[k])
+
+    def step(_, carry):
+        rz, alpha = carry
+        r = []
+        for k in range(6):
+            rhs[k, mid, :] += alpha * v[k + 1, mid, :]
+            r.append(residue[k, mid, :] - alpha * coef[k, mid, :])
+            residue[k, mid, :] = r[k]
+        z, w, rz_new, zaz = turn(r)
+        beta = rz_new / rz
+        for k in range(6):
+            v[k + 1, mid, :] = z[k] + beta * v[k + 1, mid, :]
+            coef[k, mid, :] = w[k] + beta * coef[k, mid, :]
+        return rz_new, rz_new / (zaz - beta * (rz_new / alpha))
+
+    _, alpha = lax.fori_loop(0, COARSE_ITERS - 1, step, (rz, rz / zaz))
+    for k in range(6):
+        u[k + 1, mid, :] = rhs[k, mid, :] + alpha * v[k + 1, mid, :]
 
 
 def exchanges(n0):
@@ -732,8 +746,8 @@
     for i in range(18):
         first(i)
     restrict(coef1, coef2, 18, BASE, BASE, n2, 1)
-    ex["coef1"].start([[rows_of(coef1, i) for i in range(18)]], (coef1,))
-    ex["coef2"].start([[twins_of(coef2, i) for i in range(0, 18, 2)]], (coef2,))
+    ex["coef1"].start([[rows_of(coef1, i) for i in range(18)]], (coef1,), False)
+    ex["coef2"].start([[twins_of(coef2, i) for i in range(0, 18, 2)]], (coef2,), False)
     gx, gy = lax.axis_index("gx"), lax.axis_index("gy")
     mine = (lax.rem(gx, 2), gy, gx // 2)
     for t in range(3):
@@ -743,6 +757,8 @@
     begin(coef_moves[0])
 
     edge.finish()
+    ex["coef1"].launch()
+    ex["coef2"].launch()
     edge.unpack(0, fields, [(edge.tops[0], i) for i in range(12)])
     edge.unpack(1, labs, [(edge.tops[1], i) for i in range(13)])
     lo, hi0, hi1, hi2 = BASE - HALO, BASE + n0 + HALO, BASE + n1 + HALO, BASE + n2 + HALO
@@ -804,8 +820,13 @@
     begin(rhs_moves[1])
     for i in range(LOCAL, LEVELS + 1):
         weigh(i, 8, 8 + sizes[i])
+    e = ex["rhs2"]
+    e.unpack_folded(1, [(u1, k + 1) for k in range(6)], [(e.tops[1], k) for k in range(6)])
+    e = ex["rhs1"]
+    e.unpack_folded(1, fields, [(e.tops[1], i) for i in range(12)])
     end(rhs_moves[1])
     begin(rhs_moves[2])
+    fill("u2", u2, 6, 1)
     end(rhs_moves[2])
     place(gathered_rhs, [(levels[3][2], 0)], h)
 
@@ -813,7 +834,7 @@
         smooth(levels[i], 8, 8 + sizes[i], True)
         residual(levels[i], temp3, 8, 8 + sizes[i])
         restrict(temp3, levels[i + 1][2], 6, 8, 8, sizes[i + 1], levels[i][-1])
-    conjugate(levels[LEVELS], temp3, levels[LEVELS][2])
+    conjugate(levels[LEVELS], temp3)
     for i in reversed(range(LOCAL, LEVELS)):
         prolong(levels[i + 1][0], levels[i][0], 8, sizes[i + 1], 8, levels[i][-1])
         smooth(levels[i], 8, 8 + sizes[i], False)
@@ -824,7 +845,6 @@
     c = lax.broadcasted_iota(jnp.int32, (columns, LANES), 1)
     hit = ((c & 1) == 0) & (c // 4 - LEFT // 4 + gy * 16 == r)
     widen = chosen(hit)
-    fill("u2", u2, 6, 1)
 
     for k in range(6):
         x = u3[k + 1, pl.ds(pl.multiple_of(gx * h, 8), h + 16), :]
@@ -832,12 +852,8 @@
         u2[k + 1, pl.ds(0, h + 16, 2), :] += x
         u2[k + 1, pl.ds(1, h + 16, 2), :] += x
     smooth(levels[2], lo, hi2, False)
-    e = ex["rhs2"]
-    e.unpack_folded(1, [(u1, k + 1) for k in range(6)], [(e.tops[1], k) for k in range(6)])
     prolong(u2, u1, lo, n2 + 16, 0, 1)
     smooth(levels[1], lo, hi1, False)
-    e = ex["rhs1"]
-    e.unpack_folded(1, fields, [(e.tops[1], i) for i in range(12)])
 
     for k in range(6):
         x = u1[k + 1, lo : lo + n1 + 16, :]

time: 55.6 us -> 53 us (0.953)
  Pallas kernels: 53.7 us -> 51.1 us
    pallas_call x1, Pallas kernels: 53.7 us -> 51.1 us  [on_device(): pl.pallas_call(whole_kernel, out_shape=jax.ShapeDtypeStruct(field.shape,...]
where the time goes in v5:
time: 53 us; the launch traced here: 52.9 us
  Pallas kernels  51.1 us (96%)
  local copies, waits for them, and re-layouts  1.77 us (3%)
    pallas_call x1, Pallas kernels, on_device(): pl.pallas_call(whole_kernel, out_shape=jax.ShapeDtypeStruct(field.shape,...  51.1 us
    unnamed x1, local copies, waits for them, and re-layouts  1.77 us

profile of v5, /device:TPU:0, one launch (start us, length us, event | category | flops | bytes accessed | tf_op | source)
XLA Modules:
  0.0 52.9 jit_solution(16480378557469007770)
XLA Ops:
  0.0 51.1 %shard_map.73 = f32[6,128,128]{2,1,0:T(8,128)} custom-call(f32[6,128,128]{2,1,0:T(8,128)} %field.1, s32[6,128,128]{2,1,0:T(8,128)} %labels.1, s32[8,8]{1,0:T(8,128)} %patch.1, f32[8]{0:T(128)} %lat_t.1, f32[8]{0:T(128)} %ver_t.1, f32[8]{0:T(128)} %sto_t.1, f32[64]{0:T(128)} %wattage.1), custom_call_target="tpu_custom_call" | custom-call | tf_op jit(solution)/shard_map/pallas_call | solution.py:889
  51.1 1.8 %copy.9 = f32[6,128,128]{2,1,0:T(8,128)} copy(f32[6,128,128]{2,1,0:T(8,128)} %shard_map.73) | data formatting | bytes 786432

commit v6 on v5

--- a/solution.py
+++ b/solution.py
@@ -579,7 +579,8 @@
     n = u.shape[1] - 16
     mid = slice(8, 8 + n)
 
-    def summed(x):
+    def dot(x, y):
+        x = [a * b for a, b in zip(x, y)]
         total = (x[0] + x[1]) + (x[2] + x[3]) + (x[4] + x[5])
         return jnp.sum(jnp.sum(total, axis=0, keepdims=True), axis=1, keepdims=True)
 
@@ -591,11 +592,10 @@
             coef[12 + k, mid, :] * z[k] - beside(u, wr, wc, wv, gap, k, 8, n, z[k])
             for k in range(6)
         ]
-        rz = summed([a * b for a, b in zip(r, z)])
-        return z, w, rz, summed([a * b for a, b in zip(w, z)])
+        return z, w, dot(r, z)
 
     r = [rhs[k, mid, :] for k in range(6)]
-    z, w, rz, zaz = turn(r)
+    z, w, rz = turn(r)
     for k in range(6):
         residue[k, mid, :] = r[k]
         v[k + 1, mid, :] = z[k]
@@ -609,14 +609,16 @@
             rhs[k, mid, :] += alpha * v[k + 1, mid, :]
             r.append(residue[k, mid, :] - alpha * coef[k, mid, :])
             residue[k, mid, :] = r[k]
-        z, w, rz_new, zaz = turn(r)
+        z, w, rz_new = turn(r)
         beta = rz_new / rz
+        p = [z[k] + beta * v[k + 1, mid, :] for k in range(6)]
+        q = [w[k] + beta * coef[k, mid, :] for k in range(6)]
         for k in range(6):
-            v[k + 1, mid, :] = z[k] + beta * v[k + 1, mid, :]
-            coef[k, mid, :] = w[k] + beta * coef[k, mid, :]
-        return rz_new, rz_new / (zaz - beta * (rz_new / alpha))
-
-    _, alpha = lax.fori_loop(0, COARSE_ITERS - 1, step, (rz, rz / zaz))
+            v[k + 1, mid, :] = p[k]
+            coef[k, mid, :] = q[k]
+        return rz_new, rz_new / dot(p, q)
+
+    _, alpha = lax.fori_loop(0, COARSE_ITERS - 1, step, (rz, rz / dot(z, w)))
     for k in range(6):
         u[k + 1, mid, :] = rhs[k, mid, :] + alpha * v[k + 1, mid, :]
 

time: 53 us -> 53.2 us (level)
  no operation moved by 1% of the time
where the time goes in v6:
time: 53.2 us; the launch traced here: 53.1 us
  Pallas kernels  51.3 us (96%)
  local copies, waits for them, and re-layouts  1.77 us (3%)
    pallas_call x1, Pallas kernels, on_device(): pl.pallas_call(whole_kernel, out_shape=jax.ShapeDtypeStruct(field.shape,...  51.3 us
    unnamed x1, local copies, waits for them, and re-layouts  1.77 us

profile of v6, /device:TPU:0, one launch (start us, length us, event | category | flops | bytes accessed | tf_op | source)
XLA Modules:
  0.0 53.1 jit_solution(1574427566907672900)
XLA Ops:
  0.0 51.3 %shard_map.73 = f32[6,128,128]{2,1,0:T(8,128)} custom-call(f32[6,128,128]{2,1,0:T(8,128)} %field.1, s32[6,128,128]{2,1,0:T(8,128)} %labels.1, s32[8,8]{1,0:T(8,128)} %patch.1, f32[8]{0:T(128)} %lat_t.1, f32[8]{0:T(128)} %ver_t.1, f32[8]{0:T(128)} %sto_t.1, f32[64]{0:T(128)} %wattage.1), custom_call_target="tpu_custom_call" | custom-call | tf_op jit(solution)/shard_map/pallas_call | solution.py:891
  51.3 1.8 %copy.9 = f32[6,128,128]{2,1,0:T(8,128)} copy(f32[6,128,128]{2,1,0:T(8,128)} %shard_map.73) | data formatting | bytes 786432
